TPU v7x, 512 devices: a whole 4x4x16 slice. The times are simulated.
512 devices in a mesh: mem: 32 (over z_hi, x, core), lat: 16 (over y, z_lo).
Axes of the slice: x: 4, y: 4, z: 16 (z_hi: 4, z_lo: 4; z = z_hi * 4 + z_lo), core: 2. Of those that a mesh axis runs over, the one named last changes fastest.
Arguments:
- fields: float32 [1024, 128, 256], P('mem', 'lat'), may hold values from -8 to 8
- forcing: float32 [128, 256], P('lat'), may hold values from 2 to 8
- obs_cell: int32 [16, 32, 256], P('lat'), may hold values from 0 to 63
- obs_count: int32 [16, 32], P('lat', 'mem'), may hold values from 64 to 256, as said below
- obs_value: float32 [16, 32, 256], P('lat', 'mem'), may hold values from -12 to 12
- obs_var: float32 [16, 32, 256], P('lat', 'mem'), may hold values from 0.25 to 1
Outputs:
- analysis: float32 [1024, 128, 256], P('mem', 'lat')
Inputs may be any that keep to these rules, and one draw needn't show every extreme that they name: `obs_count`: each latitude strip has a patch with exactly 256 live observations.
All inputs are finite; a program needn't handle non-finite values.
Results may differ from a plain program's by a relative error of at most 0.0003.
Values sent between devices are 32-bit elements; how exact they have to be, the bound alone decides.
No kernel may reach another device: no remote copies, remote signals or barrier semaphores. Data moves between devices by JAX's collectives and lax.ppermute only.
A program may use at most 64 MiB of HBM per device.

v0:
```python
import jax
import jax.numpy as jnp
from jax import lax
from jax.sharding import PartitionSpec as P

PATCH_CELLS = 64
STEPS = 4


TIME_STEP = 0.05
LAT_MIXING = 4.0


def with_halo(value, sides, width):
    for axis, dim in sides:
        size, length = (lax.axis_size(axis), value.shape[dim])
        up = [(i, (i + 1) % size) for i in range(size - 1)]
        down = [(j, i) for i, j in up]
        last = lax.slice_in_dim(value, length - width, length, axis=dim)
        leading = lax.slice_in_dim(value, 0, width, axis=dim)
        before = lax.ppermute(last, axis, up)
        after = lax.ppermute(leading, axis, down)
        value = jnp.concatenate([before, value, after], axis=dim)
    return value


def advance(middle, upper, lower, forcing):
    eastern = jnp.roll(middle, -1, axis=2)
    western = jnp.roll(middle, 1, axis=2)
    far_west = jnp.roll(middle, 2, axis=2)
    tendency = (
        (eastern - far_west) * western
        - middle
        + forcing
        + LAT_MIXING * (upper + lower - 2.0 * middle)
    )
    return middle + TIME_STEP * tendency


def analyse(patch_cells, observed, live_count, values, variances):
    members = patch_cells.shape[1]
    anomalies = patch_cells - jnp.mean(patch_cells, axis=1, keepdims=True)
    mean_obs = jnp.mean(observed, axis=1, keepdims=True)
    live = (jnp.arange(observed.shape[0]) < live_count)[:, None]
    obs_anom = jnp.where(live, observed - mean_obs, jnp.float32(0.0))
    gram = jnp.dot(obs_anom, obs_anom.T, precision=lax.Precision.HIGHEST) / (members - 1)
    gram = gram + jnp.diag(jnp.where(live[:, 0], variances, jnp.float32(1.0)))
    innovation = jnp.where(live, values[:, None] - mean_obs, jnp.float32(0.0))
    target = innovation - 0.5 * obs_anom
    factor = jnp.linalg.cholesky(gram)
    solved = jax.scipy.linalg.cho_solve((factor, True), target)
    cross = jnp.dot(anomalies, obs_anom.T, precision=lax.Precision.HIGHEST) / (members - 1)
    return patch_cells + jnp.dot(cross, solved, precision=lax.Precision.HIGHEST)


def local(fields, forcing, obs_cell, obs_count, obs_value, obs_var):
    group_size, rows_dev, lon_cells = fields.shape
    stacked = jnp.concatenate([fields, forcing[None]], axis=0)
    extended = with_halo(stacked, (("lat", 1),), STEPS)
    current = extended[:-1]
    row_forcing = extended[-1]
    for repeat_index in range(STEPS):
        updated = advance(current[:, 1:-1], current[:, 2:], current[:, :-2], row_forcing[1:-1])
        margin = STEPS - repeat_index - 1
        global_rows = lax.axis_index("lat") * rows_dev - margin + jnp.arange(updated.shape[1])
        inside = (global_rows >= 0) & (global_rows < lax.axis_size("lat") * rows_dev)
        current = jnp.where(inside[None, :, None], updated, jnp.float32(0.0))
        row_forcing = row_forcing[1:-1]
    strip_cells = rows_dev * lon_cells
    flat_fields = current.reshape(group_size, strip_cells)
    patch_dev = obs_count.shape[1]
    first_patch = lax.axis_index("mem") * patch_dev
    local_cells = lax.dynamic_slice_in_dim(obs_cell[0], first_patch, patch_dev, 0)
    gathered = lax.all_to_all(flat_fields, "mem", split_axis=1, concat_axis=0, tiled=True)
    members = gathered.shape[0]
    patches = gathered.T.reshape(patch_dev, PATCH_CELLS, members)
    observed = jax.vmap(lambda cells, index: jnp.take(cells, index, axis=0))(patches, local_cells)

    def one_patch(items):
        patch_cells, patch_observed, live_count, values, variances = items
        return analyse(patch_cells, patch_observed, live_count, values, variances)

    result = lax.map(one_patch, (patches, observed, obs_count[0], obs_value[0], obs_var[0]))
    outgoing = result.reshape(patch_dev * PATCH_CELLS, members).T
    returned = lax.all_to_all(outgoing, "mem", split_axis=0, concat_axis=1, tiled=True)
    return returned.reshape(group_size, rows_dev, lon_cells)


def solution(mesh):
    placed = (
        P("mem", "lat", None),
        P("lat", None),
        P("lat", None, None),
        P("lat", "mem"),
        P("lat", "mem", None),
        P("lat", "mem", None),
    )
    return jax.shard_map(
        local, mesh=mesh, in_specs=placed, out_specs=P("mem", "lat", None), check_vma=False
    )
```

profile of v0, /device:TPU:1, one launch (start us, length us, event | category | flops | bytes accessed | tf_op | source)
XLA Modules:
  0.0 163.3 jit_solution(11233536615849166927)
XLA Ops:
  0.0 1.1 fusion.55
  1.2 4.4 %collective-permute-start = (f32[33,4,256]{2,1,0:T(4,128)S(1)}, f32[33,4,256]{2,1,0:T(4,128)S(1)}, u32[]{:S(2)}, u32[]{:S(2)}) collective-permute-start(f32[33,4,256]{2,1,0:T(4,128)S(1)} %get-tuple-element.62), channel_id=1, source_target_pairs={{0,1},{1,2},{2,3},{3,4},{4,5},{5,6},{6,7},{7,8},{8,9},{9,10},{10,1... | collective-permute-start | bytes 405512 | tf_op jit(solution)/shard_map/ppermute | solution.py:21
  5.5 1.3 collective-permute-start.1
  7.5 6.0 %collective-permute-done.1 = f32[33,4,256]{2,1,0:T(4,128)S(1)} collective-permute-done((f32[33,4,256]{2,1,0:T(4,128)S(1)}, f32[33,4,256]{2,1,0:T(4,128)S(1)}, u32[]{:S(2)}, u32[]{:S(2)}) %collective-permute-start.1) | collective-permute-done | bytes 135200 | tf_op jit(solution)/shard_map/ppermute | solution.py:22
  18.1 1.0 reshape.325
  19.1 19.8 %all-to-all-start = ((f32[32,1,2048]{2,1,0:T(1,128)}), f32[32,1,2048]{2,1,0:T(1,128)S(1)}, u32[]{:S(2)}, u32[]{:S(2)}) async-start(f32[32,1,2048]{2,1,0:T(1,128)} %reshape.325), calls=%async_computation | async-start | bytes 524288 | tf_op jit(solution)/shard_map/all_to_all | solution.py:74
  39.6 0.7 compare_select_fusion
  40.4 18.9 %all-to-all-done = f32[32,1,2048]{2,1,0:T(1,128)S(1)} async-done(((f32[32,1,2048]{2,1,0:T(1,128)}), f32[32,1,2048]{2,1,0:T(1,128)S(1)}, u32[]{:S(2)}, u32[]{:S(2)}) %all-to-all-start) | async-done | bytes 262176 | tf_op jit(solution)/shard_map/all_to_all | solution.py:74
  59.8 1.3 reduce.19
  61.6 2.0 %gather_fusion = f32[256,1024]{1,0:T(8,128)S(1)} fusion(f32[1,64,1024]{2,1,0:T(8,128)S(1)} %bitcast.79, s32[256]{0:T(256)S(1)} %bitcast.80), kind=kCustom, calls=%fused_computation | custom fusion | bytes 2099200 | tf_op jit(solution)/shard_map/vmap(jit(_take))/gather | solution.py:77
  64.5 1.3 convolution_multiply_fusion
  65.9 1.2 convolution_multiply_fusion.1
  67.6 11.7 %cholesky.49 = f32[128,128]{1,0:T(8,128)S(1)} custom-call(f32[128,128]{1,0:T(8,128)S(1)} %cholesky.115), custom_call_target="Cholesky" | custom-call | tf_op jit(solution)/shard_map/while/body/eval_jaxpr/jit(cholesky)/cholesky | solution.py:50
  80.0 9.8 %custom-call.22 = f32[1,128,128]{1,2,0:T(8,128)S(1)} custom-call(f32[1,128,128]{2,1,0:T(8,128)S(1)} %get-tuple-element.67), custom_call_target="InvertDiagBlocksLowerTriangular" | custom-call | tf_op jit(solution)/shard_map/while/body/eval_jaxpr/jit(cholesky)/cholesky | solution.py:50
  90.4 11.9 %cholesky.103 = f32[128,128]{1,0:T(8,128)S(1)} custom-call(f32[128,128]{1,0:T(8,128)S(1)} %convolution_subtract_fusion.2), custom_call_target="Cholesky" | custom-call | tf_op jit(solution)/shard_map/while/body/eval_jaxpr/jit(cholesky)/cholesky | solution.py:50
  102.3 0.7 compare_reduce_fusion
  104.4 4.0 %while.1 = (s32[]{:T(128)}, f32[256,256]{1,0:T(8,128)S(1)}, s32[2,2]{1,0:T(2,128)S(1)}, f32[2,128,128]{2,1,0:T(8,128)S(1)}, s32[]{:T(128)}) while((s32[]{:T(128)}, f32[256,256]{1,0:T(8,128)S(1)}, s32[2,2]{1,0:T(2,128)S(1)}, f32[2,128,128]{2,1,0:T(8,128)S(1)}, s32[]{:T(128)}) %tuple.36), condition=%wide.while_cond, body=%wide.while_body.sunk | while | flops 2 | bytes 131189 | solution.py:51
  105.0 1.4 bitcast_dynamic-update-slice_fusion.2
  107.0 1.4 bitcast_dynamic-update-slice_fusion.2
  108.4 19.7 %custom-call.23 = f32[2,128,128]{1,2,0:T(8,128)S(1)} custom-call(f32[2,128,128]{2,1,0:T(8,128)S(1)} %get-tuple-element.33), custom_call_target="InvertDiagBlocksLowerTriangular" | custom-call | tf_op jit(solution)/shard_map/while/body/eval_jaxpr/jit(_cho_solve)/triangular_solve | solution.py:51
  131.8 0.8 convolution_add_fusion
  133.1 27.5 %all_to_all.35 = f32[32,1,2048]{2,1,0:T(1,128)S(1)} all-to-all(f32[32,1,2048]{2,1,0:T(1,128)S(1)} %reshape.327), channel_id=1, replica_groups=mesh['mem'=32,'lat'=16] {'mem'}, dimensions={0} | all-to-all | bytes 524288 | tf_op jit(solution)/shard_map/all_to_all | solution.py:85
  160.6 1.3 reduce.20
  162.4 0.9 reshape.295
  (78 shorter events, 14.8 us)
Async XLA Ops:
  0.0 13.5 %copy-start = (f32[32,8,256]{2,1,0:T(8,128)S(1)}, f32[32,8,256]{2,1,0:T(8,128)}, u32[]{:S(2)}) copy-start(f32[32,8,256]{2,1,0:T(8,128)} %param.6) | copy-start | bytes 786436
  1.2 6.3 %collective-permute-start = (f32[33,4,256]{2,1,0:T(4,128)S(1)}, f32[33,4,256]{2,1,0:T(4,128)S(1)}, u32[]{:S(2)}, u32[]{:S(2)}) collective-permute-start(f32[33,4,256]{2,1,0:T(4,128)S(1)} %get-tuple-element.62), channel_id=1, source_target_pairs={{0,1},{1,2},{2,3},{3,4},{4,5},{5,6},{6,7},{7,8},{8,9},{9,10},{10,1... | collective-permute-start | bytes 405512 | tf_op jit(solution)/shard_map/ppermute | solution.py:21
  5.5 8.0 %collective-permute-start.1 = (f32[33,4,256]{2,1,0:T(4,128)S(1)}, f32[33,4,256]{2,1,0:T(4,128)S(1)}, u32[]{:S(2)}, u32[]{:S(2)}) collective-permute-start(f32[33,4,256]{2,1,0:T(4,128)S(1)} %get-tuple-element.63), channel_id=1, source_target_pairs={{1,0},{2,1},{3,2},{4,3},{5,4},{6,5},{7,6},{8,7},{9,8},{10,9},{11,1... | collective-permute-start | bytes 405512 | tf_op jit(solution)/shard_map/ppermute | solution.py:22
  6.8 6.7 %copy-start.1 = (f32[8,256]{1,0:T(8,128)S(1)}, f32[8,256]{1,0:T(8,128)}, u32[]{:S(2)}) copy-start(f32[8,256]{1,0:T(8,128)} %param.7) | copy-start | bytes 24580
  19.1 40.1 %all-to-all-start = ((f32[32,1,2048]{2,1,0:T(1,128)}), f32[32,1,2048]{2,1,0:T(1,128)S(1)}, u32[]{:S(2)}, u32[]{:S(2)}) async-start(f32[32,1,2048]{2,1,0:T(1,128)} %reshape.325), calls=%async_computation | async-start | bytes 524288 | tf_op jit(solution)/shard_map/all_to_all | solution.py:74
  63.6 0.7 copy-start.3
  63.8 0.7 copy-start.2
where the time goes:
time: 165 us; the launch traced here: 163 us
  other arithmetic  61.8 us (37%)
  blocking collectives  27.5 us (17%)
  waiting for transfers between devices  25.5 us (15%)
  starting transfers between devices  25.4 us (15%)
  local copies, waits for them, and re-layouts  13.1 us (8%)
  matrix products  7.48 us (5%)
  between operations  2.43 us (1%)
    another operation x7, other arithmetic, analyse(): factor = jnp.linalg.cholesky(gram)  34.9 us
    all_to_all x1, blocking collectives, local(): lax.all_to_all(outgoing, 'mem', split_axis=0, concat_axis=1, tiled=True)  27.5 us
    all_to_all x1, starting transfers between devices, local(): lax.all_to_all(flat_fields, 'mem', split_axis=1, concat_axis=0, tiled=True)  19.8 us
    another operation x3, other arithmetic, analyse(): solved = jax.scipy.linalg.cho_solve((factor, True), target)  19.7 us
    all_to_all x1, waiting for transfers between devices, local(): lax.all_to_all(flat_fields, 'mem', split_axis=1, concat_axis=0, tiled=True)  18.9 us
    ppermute x1, waiting for transfers between devices, with_halo(): after = lax.ppermute(leading, axis, down)  6.03 us
    ppermute x1, starting transfers between devices, with_halo(): before = lax.ppermute(last, axis, up)  4.37 us
    another operation x6, local copies, waits for them, and re-layouts  3.95 us
  transfers between devices with their start and end apart: 3, of which 3 were waited for; matrix products, arithmetic and copies ran while one was open for 0% of the time, Pallas kernels for 0%

commit v1 on v0

v1 whole, which is shorter than its diff:
```python
import functools

import jax
import jax.numpy as jnp
from jax import lax
from jax.experimental import pallas as pl
from jax.experimental.pallas import tpu as pltpu
from jax.sharding import PartitionSpec as P

CELLS = 64
STEPS = 4
TIME_STEP = 0.05
LAT_MIXING = 4.0
NEAR = 8
FAR = 4
HIGHEST = lax.Precision.HIGHEST
LANES = 128
NEAR_GROUPS = [[hi * NEAR + near for near in range(NEAR)] for hi in range(FAR)]
FAR_GROUPS = [[hi * NEAR + near for hi in range(FAR)] for near in range(NEAR)]


def low_half(shape):
    return lax.broadcasted_iota(jnp.int32, shape, 1) < CELLS


def halves(left, left_half, right, right_half):
    left = left if left_half == 0 else pltpu.roll(left, CELLS, 1)
    right = right if right_half == 1 else pltpu.roll(right, CELLS, 1)
    return jnp.where(low_half(left.shape), left, right)


def pack_kernel(fields, forcing, top, bottom):
    members = fields.shape[0]
    for out, start in ((top, 0), (bottom, STEPS)):
        for row in range(STEPS):
            out[pl.ds(row * members, members), :] = fields[:, start + row, :]
        edge = forcing[pl.ds(start, STEPS), :]
        out[pl.ds(STEPS * members, 2 * STEPS), :] = jnp.concatenate([edge, edge], axis=0)


def observe_kernel(scalars, cells, values, variances, out):
    slots = values.shape[2]
    live = lax.broadcasted_iota(jnp.int32, (1, slots), 1) < scalars[1]
    weight = jnp.where(live, 1.0 / variances[0], 0.0)
    scaled = weight * values[0]
    mine = cells[0, pl.ds(scalars[0], 1), :]
    cell = lax.broadcasted_iota(jnp.int32, (2 * CELLS, slots), 0) % CELLS
    hit = jnp.where(cell == mine, 1.0, 0.0)
    row = lax.broadcasted_iota(jnp.int32, (8, slots), 0)
    terms = jnp.where(row == 0, weight, jnp.where(row == 1, scaled, 0.0))
    sums = lax.dot_general(
        terms, hit, (((1,), (1,)), ((), ())), precision=HIGHEST, preferred_element_type=jnp.float32
    )
    both = jnp.where(low_half((1, LANES)), sums[0:1], sums[1:2])
    out[...] = jnp.broadcast_to(both, (8, LANES))


def forecast_kernel(last_strip, scalars, before, top, bottom, after, out):
    members = out.shape[1]
    strip = scalars[2]
    sources = [before] * STEPS + [top] * STEPS + [bottom] * STEPS + [after] * STEPS
    for tile in range(members // 8):
        rows = [
            source[pl.ds((place % STEPS) * members + tile * 8, 8), :]
            for place, source in enumerate(sources)
        ]
        for step in range(STEPS):
            updated = []
            for inner in range(1, len(rows) - 1):
                place = step + inner
                here = rows[inner]
                force = sources[place][pl.ds(STEPS * members + place % STEPS, 1), :]
                eastern = pltpu.roll(here, here.shape[1] - 1, 1)
                western = pltpu.roll(here, 1, 1)
                far_west = pltpu.roll(here, 2, 1)
                tendency = (
                    (eastern - far_west) * western
                    - here
                    + force
                    + LAT_MIXING * (rows[inner - 1] + rows[inner + 1] - 2.0 * here)
                )
                value = here + TIME_STEP * tendency
                if place < STEPS:
                    value = jnp.where(strip == 0, 0.0, value)
                if place >= 3 * STEPS:
                    value = jnp.where(strip == last_strip, 0.0, value)
                updated.append(value)
            rows = updated
        for near in range(NEAR):
            block = near % 4
            lanes = slice(block // 2 * LANES, block // 2 * LANES + LANES)
            parts = [rows[2 * hi + near // 4][:, lanes] for hi in range(FAR)]
            half = block % 2
            out[near, pl.ds(tile * 8, 8), pl.ds(0, LANES)] = halves(parts[0], half, parts[1], half)
            out[near, pl.ds(tile * 8, 8), pl.ds(LANES, LANES)] = halves(parts[2], half, parts[3], half)


def fold(square):
    return jnp.where(low_half((CELLS, LANES)), square[:CELLS], square[CELLS:])


def moments_kernel(states, observed, out):
    lines = []
    for half in range(2):
        block = states[:, pl.ds(half * LANES, LANES)]
        mean = jnp.sum(block, axis=0, keepdims=True) / block.shape[0]
        centred = block - mean
        square = lax.dot_general(
            centred, centred, (((0,), (0,)), ((), ())), precision=HIGHEST, preferred_element_type=jnp.float32
        )
        folded = fold(square)
        for hi in range(FAR):
            out[hi, pl.ds(half * CELLS, CELLS), :] = folded
        lines.append(mean)
    row = lax.broadcasted_iota(jnp.int32, (8, LANES), 0)
    tail = jnp.where(row == 0, lines[0], jnp.where(row == 1, lines[1], observed[...]))
    for hi in range(FAR):
        out[hi, pl.ds(LANES, 8), :] = tail


def eliminate(systems):
    row = lax.broadcasted_iota(jnp.int32, (8, LANES), 0)
    for pivot in range(CELLS):
        tile, line = divmod(pivot, 8)
        for system in systems:
            factors = [jnp.broadcast_to(part[:, pivot:pivot + 1], (8, LANES)) for part in system]
            lead = jnp.broadcast_to(system[tile][line:line + 1, :], (8, LANES))
            lead = lead / jnp.broadcast_to(factors[tile][line:line + 1, :], (8, LANES))
            for place in range(8):
                rest = system[place] - factors[place] * lead
                system[place] = jnp.where(row == line, lead, rest) if place == tile else rest
    return systems


def analyse_kernel(received, states, out, gains):
    group = states.shape[0]
    members = FAR * group
    low = low_half((CELLS, LANES))
    means, covariances = [], []
    for half in range(2):
        means_far = [received[hi, pl.ds(LANES + half, 1), :] for hi in range(FAR)]
        mean = (means_far[0] + means_far[1] + means_far[2] + means_far[3]) / FAR
        row = lax.broadcasted_iota(jnp.int32, (8, LANES), 0)
        offsets = jnp.zeros((8, LANES), jnp.float32)
        for hi in range(FAR):
            offsets = jnp.where(row == hi, means_far[hi] - mean, offsets)
        between = lax.dot_general(
            offsets, offsets, (((0,), (0,)), ((), ())), precision=HIGHEST, preferred_element_type=jnp.float32
        )
        total = group * fold(between)
        for hi in range(FAR):
            total = total + received[hi, pl.ds(half * CELLS, CELLS), :]
        means.append(mean)
        covariances.append(total / (members - 1))
    observed = [received[hi, pl.ds(LANES + 2, 1), :] for hi in range(FAR)]
    diagonal = lax.broadcasted_iota(jnp.int32, (CELLS, LANES), 0) == lax.broadcasted_iota(
        jnp.int32, (CELLS, LANES), 1
    )
    systems = []
    for patch in range(FAR):
        pair = covariances[patch // 2]
        twice = halves(pair, patch % 2, pair, patch % 2)
        scale = jnp.where(low_half((1, LANES)), observed[patch], 1.0)
        system = twice * scale + jnp.where(diagonal, 1.0, 0.0)
        systems.append([system[8 * tile:8 * tile + 8] for tile in range(8)])
    eliminate(systems)
    gains[...] = jnp.zeros(gains.shape, jnp.float32)
    for patch in range(FAR):
        for tile in range(8):
            block = systems[patch][tile]
            if patch % 2 == 0:
                block = pltpu.roll(block, CELLS, 1)
            keep = low_half((8, LANES)) if patch % 2 == 0 else jnp.logical_not(low_half((8, LANES)))
            rows = pl.ds(patch * CELLS + 8 * tile, 8)
            gains[rows, pl.ds(patch // 2 * LANES, LANES)] = jnp.where(keep, block, 0.0)
    for half in range(2):
        first, second = observed[2 * half], observed[2 * half + 1]
        weight = halves(first, 0, second, 0)
        source = halves(first, 1, second, 1)
        block = states[:, pl.ds(half * LANES, LANES)]
        mean = means[half]
        residual = (source - weight * mean) - (0.5 * weight) * (block - mean)
        square = gains[pl.ds(half * LANES, LANES), pl.ds(half * LANES, LANES)]
        out[:, pl.ds(half * LANES, LANES)] = block + jnp.dot(
            residual, square, precision=HIGHEST, preferred_element_type=jnp.float32
        )


def unpack_kernel(arrived, out):
    for row in range(out.shape[1]):
        hi, side = divmod(row, 2)
        lanes = pl.ds(hi // 2 * LANES, LANES)
        for pair in range(2):
            near = 4 * side + 2 * pair
            joined = halves(arrived[near, :, lanes], hi % 2, arrived[near + 1, :, lanes], hi % 2)
            out[:, row, pl.ds(pair * LANES, LANES)] = joined


VMEM = pl.BlockSpec(memory_space=pltpu.VMEM)
SMEM = pl.BlockSpec(memory_space=pltpu.SMEM)


def call(kernel, outs, in_specs, args, scratch=(), flops=1_000_000):
    many = isinstance(outs, list)
    shapes = [jax.ShapeDtypeStruct(s, jnp.float32) for s in (outs if many else [outs])]
    return pl.pallas_call(
        kernel,
        out_shape=shapes if many else shapes[0],
        in_specs=in_specs,
        out_specs=[VMEM] * len(shapes) if many else VMEM,
        scratch_shapes=list(scratch),
        compiler_params=pltpu.CompilerParams(vmem_limit_bytes=8 * 1024 * 1024),
        cost_estimate=pl.CostEstimate(flops=flops, bytes_accessed=500_000, transcendentals=0),
    )(*args)


def local(fields, forcing, obs_cell, obs_count, obs_value, obs_var):
    members, rows, lon = fields.shape
    strips = lax.axis_size("lat")
    scalars = jnp.stack([lax.axis_index("mem"), obs_count[0, 0], lax.axis_index("lat")]).astype(jnp.int32)
    height = STEPS * members + 2 * STEPS
    top, bottom = call(pack_kernel, [(height, lon)] * 2, [VMEM, VMEM], (fields, forcing))
    up = [(i, i + 1) for i in range(strips - 1)]
    down = [(j, i) for i, j in up]
    before = lax.ppermute(bottom, "lat", up)
    after = lax.ppermute(top, "lat", down)
    observed = call(observe_kernel, (8, LANES), [SMEM, VMEM, VMEM, VMEM], (scalars, obs_cell, obs_value, obs_var))
    states = call(
        functools.partial(forecast_kernel, strips - 1),
        (NEAR, members, lon),
        [SMEM, VMEM, VMEM, VMEM, VMEM],
        (scalars, before, top, bottom, after),
    )
    states = lax.all_to_all(states, "mem", 0, 0, axis_index_groups=NEAR_GROUPS, tiled=True)
    states = states.reshape(NEAR * members, lon)
    partial = call(moments_kernel, (FAR, LANES + 8, LANES), [VMEM, VMEM], (states, observed))
    received = lax.all_to_all(partial, "mem", 0, 0, axis_index_groups=FAR_GROUPS, tiled=True)
    result = call(
        analyse_kernel, states.shape, [VMEM, VMEM], (received, states), [pltpu.VMEM((2 * LANES, 2 * LANES), jnp.float32)]
    )
    result = result.reshape(NEAR, members, lon)
    result = lax.all_to_all(result, "mem", 0, 0, axis_index_groups=NEAR_GROUPS, tiled=True)
    return call(unpack_kernel, (members, rows, lon), [VMEM], (result,))


def solution(mesh):
    placed = (
        P("mem", "lat", None),
        P("lat", None),
        P("lat", None, None),
        P("lat", "mem"),
        P("lat", "mem", None),
        P("lat", "mem", None),
    )
    return jax.shard_map(local, mesh=mesh, in_specs=placed, out_specs=P("mem", "lat", None), check_vma=False)
```

time: 165 us -> 86.9 us (0.53)
  other arithmetic: 61.8 us -> 0.08 us
  blocking collectives: 27.5 us -> 44.5 us
  Pallas kernels: 0 us -> 15.1 us
  waiting for transfers between devices: 25.5 us -> 11.8 us
  starting transfers between devices: 25.4 us -> 12.3 us
  local copies, waits for them, and re-layouts: 13.1 us -> 1.66 us
  matrix products: 7.48 us -> 0 us
  between operations: 2.43 us -> 0.7 us
    another operation x10 -> x1, other arithmetic: 54.6 us -> 0.08 us  [local(): jnp.stack([lax.axis_index('mem'), obs_count[0, 0], lax.axis_index('lat')])]
    all_to_all x1 -> x2, blocking collectives: 27.5 us -> 44.5 us  [the longest x1 29 us: local(): lax.all_to_all(partial, 'mem', 0, 0, axis_index_groups=FAR_GROUPS, tiled=...]
    pallas_call x0 -> x6, Pallas kernels: none -> 15.1 us  [call(): pl.pallas_call(kernel, out_shape=shapes if many else shapes[0], in_specs=...]
    all_to_all x1, starting transfers between devices: 19.8 us -> 6.61 us  [local(): lax.all_to_all(states, 'mem', 0, 0, axis_index_groups=NEAR_GROUPS, tiled=...]
    all_to_all x1, waiting for transfers between devices: 18.9 us -> 5.71 us  [local(): lax.all_to_all(states, 'mem', 0, 0, axis_index_groups=NEAR_GROUPS, tiled=...]
    another operation x8 -> x0, matrix products: 4.12 us -> none  [the longest x6 3.64 us: analyse(): solved = jax.scipy.linalg.cho_solve((factor, True), target)]
    another operation x9 -> x0, local copies, waits for them, and re-layouts: 4.05 us -> none
    dot_general x3 -> x0, matrix products: 3.36 us -> none  [the longest x1 1.35 us: analyse(): jnp.dot(obs_anom, obs_anom.T, precision=lax.Precision.HIGHEST)]
  transfers between devices with their start and end apart: 3 -> 3, of which waited for: 3 -> 2; matrix products, arithmetic and copies ran while one was open for 0% -> 0% of each run, Pallas kernels for 0% -> 1%
where the time goes in v1:
time: 86.9 us; the launch traced here: 86.1 us
  blocking collectives  44.5 us (51%)
  Pallas kernels  15.1 us (17%)
  starting transfers between devices  12.3 us (14%)
  waiting for transfers between devices  11.8 us (14%)
  local copies, waits for them, and re-layouts  1.66 us (2%)
    all_to_all x1, blocking collectives, local(): lax.all_to_all(partial, 'mem', 0, 0, axis_index_groups=FAR_GROUPS, tiled=...  29 us
    all_to_all x1, blocking collectives, local(): lax.all_to_all(result, 'mem', 0, 0, axis_index_groups=NEAR_GROUPS, tiled=...  15.5 us
    pallas_call x6, Pallas kernels, call(): pl.pallas_call(kernel, out_shape=shapes if many else shapes[0], in_specs=...  15.1 us
    all_to_all x1, starting transfers between devices, local(): lax.all_to_all(states, 'mem', 0, 0, axis_index_groups=NEAR_GROUPS, tiled=...  6.61 us
    ppermute x1, waiting for transfers between devices, local(): after = lax.ppermute(top, 'lat', down)  6.09 us
    all_to_all x1, waiting for transfers between devices, local(): lax.all_to_all(states, 'mem', 0, 0, axis_index_groups=NEAR_GROUPS, tiled=...  5.71 us
    ppermute x1, starting transfers between devices, local(): before = lax.ppermute(bottom, 'lat', up)  4.37 us
  transfers between devices with their start and end apart: 3, of which 2 were waited for; matrix products, arithmetic and copies ran while one was open for 0% of the time, Pallas kernels for 1%

profile of v1, /device:TPU:1, one launch (start us, length us, event | category | flops | bytes accessed | tf_op | source)
XLA Modules:
  0.0 86.1 jit_solution(17281773111507573251)
XLA Ops:
  0.0 0.0 copy-start
  0.0 0.9 %copy-done = f32[32,8,256]{2,1,0:T(8,128)S(1)} copy-done((f32[32,8,256]{2,1,0:T(8,128)S(1)}, f32[32,8,256]{2,1,0:T(8,128)}, u32[]{:S(2)}) %copy-start) | copy-done | bytes 262168
  1.0 0.0 copy-start.2
  1.0 0.7 copy-done.2
  1.6 0.1 shard_map.64
  1.7 4.4 %collective-permute-start = (f32[136,256]{1,0:T(8,128)S(1)}, f32[136,256]{1,0:T(8,128)S(1)}, u32[]{:S(2)}, u32[]{:S(2)}) collective-permute-start(f32[136,256]{1,0:T(8,128)S(1)} %get-tuple-element.7.bottom), channel_id=1, source_target_pairs={{0,1},{1,2},{2,3},{3,4},{4,5},{5,6},{6,7},{7,8},{8,9},{9,10},{10,1... | collective-permute-start | bytes 417800 | tf_op jit(solution)/shard_map/ppermute | solution.py:225
  6.1 1.3 %collective-permute-start.1 = (f32[136,256]{1,0:T(8,128)S(1)}, f32[136,256]{1,0:T(8,128)S(1)}, u32[]{:S(2)}, u32[]{:S(2)}) collective-permute-start(f32[136,256]{1,0:T(8,128)S(1)} %get-tuple-element.8.top), channel_id=1, source_target_pairs={{1,0},{2,1},{3,2},{4,3},{5,4},{6,5},{7,6},{8,7},{9,8},{10,9},{11,1... | collective-permute-start | bytes 417800 | tf_op jit(solution)/shard_map/ppermute | solution.py:226
  8.1 0.1 pad_add_fusion.scalars
  8.1 0.0 collective-permute-done.before
  8.1 6.1 %collective-permute-done.1.after = f32[136,256]{1,0:T(8,128)S(1)} collective-permute-done((f32[136,256]{1,0:T(8,128)S(1)}, f32[136,256]{1,0:T(8,128)S(1)}, u32[]{:S(2)}, u32[]{:S(2)}) %collective-permute-start.1) | collective-permute-done | bytes 139296 | tf_op jit(solution)/shard_map/ppermute | solution.py:226
  14.2 2.9 %shard_map.65 = f32[8,32,256]{2,1,0:T(8,128)} custom-call(s32[3]{0:T(128)S(1)} %pad_add_fusion.scalars, f32[136,256]{1,0:T(8,128)S(1)} %collective-permute-done.before, f32[136,256]{1,0:T(8,128)S(1)} %get-tuple-element.8.top, f32[136,256]{1,0:T(8,128)S(1)} %get-tuple-element.7.bottom, f32[136,256]{1,0:T(8,128)S(1)} %collective-permute-done.1.after), custom_call_target="tpu_custom_call" | custom-call | flops 1000000 | bytes 500000 | tf_op jit(solution)/shard_map/pallas_call | solution.py:206
  17.2 0.0 copy-start.1
  17.2 0.0 copy-start.3
  17.2 6.6 %all-to-all-start = ((f32[8,32,256]{2,1,0:T(8,128)}), f32[8,32,256]{2,1,0:T(8,128)S(1)}, u32[]{:S(2)}, u32[]{:S(2)}) async-start(f32[8,32,256]{2,1,0:T(8,128)} %shard_map.65), calls=%async_computation | async-start | bytes 524288 | tf_op jit(solution)/shard_map/all_to_all | solution.py:234
  23.8 0.0 copy-done.1
  23.8 0.0 copy-done.3
  23.8 0.0 copy-done.4
  23.8 0.7 shard_map.66.observed
  24.5 5.7 %all-to-all-done = f32[8,32,256]{2,1,0:T(8,128)S(1)} async-done(((f32[8,32,256]{2,1,0:T(8,128)}), f32[8,32,256]{2,1,0:T(8,128)S(1)}, u32[]{:S(2)}, u32[]{:S(2)}) %all-to-all-start) | async-done | bytes 262176 | tf_op jit(solution)/shard_map/all_to_all | solution.py:234
  30.2 0.5 shard_map.67
  30.7 29.0 %all_to_all.15.received = f32[4,136,128]{2,1,0:T(8,128)S(1)} all-to-all(f32[4,136,128]{2,1,0:T(8,128)S(1)} %shard_map.67), channel_id=1, replica_groups={{0,128,256,384},{16,144,272,400},{32,160,288,416},{48,176,304,432},{64,..., dimensions={0} | all-to-all | bytes 557056 | tf_op jit(solution)/shard_map/all_to_all | solution.py:237
  59.7 9.9 %shard_map.68 = f32[256,256]{1,0:T(8,128)S(1)} custom-call(f32[4,136,128]{2,1,0:T(8,128)S(1)} %all_to_all.15.received, f32[256,256]{1,0:T(8,128)S(1)} %bitcast.7), custom_call_target="tpu_custom_call" | custom-call | flops 1000000 | bytes 500000 | tf_op jit(solution)/shard_map/pallas_call | solution.py:206
  69.6 15.5 %all_to_all.16.arrived = f32[8,32,256]{2,1,0:T(8,128)S(1)} all-to-all(f32[8,32,256]{2,1,0:T(8,128)S(1)} %bitcast.8), channel_id=1, replica_groups={{0,16,32,48,64,80,96,112},{128,144,160,176,192,208,224,240},{256,272,28..., dimensions={0} | all-to-all | bytes 524288 | tf_op jit(solution)/shard_map/all_to_all | solution.py:242
  85.2 0.9 %shard_map.69 = f32[32,8,256]{2,1,0:T(8,128)} custom-call(f32[8,32,256]{2,1,0:T(8,128)S(1)} %all_to_all.16.arrived), custom_call_target="tpu_custom_call" | custom-call | flops 1000000 | bytes 500000 | tf_op jit(solution)/shard_map/pallas_call | solution.py:206
  (1 shorter events, 0.0 us)
Async XLA Ops:
  0.0 0.9 %copy-start = (f32[32,8,256]{2,1,0:T(8,128)S(1)}, f32[32,8,256]{2,1,0:T(8,128)}, u32[]{:S(2)}) copy-start(f32[32,8,256]{2,1,0:T(8,128)} %fields.1) | copy-start | bytes 786436
  1.0 0.7 copy-start.2
  1.7 6.4 %collective-permute-start = (f32[136,256]{1,0:T(8,128)S(1)}, f32[136,256]{1,0:T(8,128)S(1)}, u32[]{:S(2)}, u32[]{:S(2)}) collective-permute-start(f32[136,256]{1,0:T(8,128)S(1)} %get-tuple-element.7.bottom), channel_id=1, source_target_pairs={{0,1},{1,2},{2,3},{3,4},{4,5},{5,6},{6,7},{7,8},{8,9},{9,10},{10,1... | collective-permute-start | bytes 417800 | tf_op jit(solution)/shard_map/ppermute | solution.py:225
  6.1 8.1 %collective-permute-start.1 = (f32[136,256]{1,0:T(8,128)S(1)}, f32[136,256]{1,0:T(8,128)S(1)}, u32[]{:S(2)}, u32[]{:S(2)}) collective-permute-start(f32[136,256]{1,0:T(8,128)S(1)} %get-tuple-element.8.top), channel_id=1, source_target_pairs={{1,0},{2,1},{3,2},{4,3},{5,4},{6,5},{7,6},{8,7},{9,8},{10,9},{11,1... | collective-permute-start | bytes 417800 | tf_op jit(solution)/shard_map/ppermute | solution.py:226
  17.2 6.6 %copy-start.1 = (s32[1,32,256]{2,1,0:T(8,128)S(1)}, s32[1,32,256]{2,1,0:T(8,128)}, u32[]{:S(2)}) copy-start(s32[1,32,256]{2,1,0:T(8,128)} %cells.1) | copy-start | bytes 98308
  17.2 6.6 %copy-start.3 = (f32[1,1,256]{2,1,0:T(1,128)S(1)}, f32[1,1,256]{2,1,0:T(1,128)}, u32[]{:S(2)}) copy-start(f32[1,1,256]{2,1,0:T(1,128)} %values.1) | copy-start | bytes 3076
  17.2 6.6 %copy-start.4 = (f32[1,1,256]{2,1,0:T(1,128)S(1)}, f32[1,1,256]{2,1,0:T(1,128)}, u32[]{:S(2)}) copy-start(f32[1,1,256]{2,1,0:T(1,128)} %variances.1) | copy-start | bytes 3076
  17.2 13.1 %all-to-all-start = ((f32[8,32,256]{2,1,0:T(8,128)}), f32[8,32,256]{2,1,0:T(8,128)S(1)}, u32[]{:S(2)}, u32[]{:S(2)}) async-start(f32[8,32,256]{2,1,0:T(8,128)} %shard_map.65), calls=%async_computation | async-start | bytes 524288 | tf_op jit(solution)/shard_map/all_to_all | solution.py:234

commit v2 on v1

v2 whole, which is shorter than its diff:
```python
import functools

import jax
import jax.numpy as jnp
from jax import lax
from jax.experimental import pallas as pl
from jax.experimental.pallas import tpu as pltpu
from jax.sharding import PartitionSpec as P

CELLS = 64
STEPS = 4
TIME_STEP = 0.05
LAT_MIXING = 4.0
NEAR = 8
FAR = 4
HIGHEST = lax.Precision.HIGHEST
LANES = 128
NEAR_GROUPS = [[hi * NEAR + near for near in range(NEAR)] for hi in range(FAR)]
FAR_GROUPS = [[hi * NEAR + near for hi in range(FAR)] for near in range(NEAR)]


def low_half(shape):
    return lax.broadcasted_iota(jnp.int32, shape, 1) < CELLS


def halves(left, left_half, right, right_half):
    left = left if left_half == 0 else pltpu.roll(left, CELLS, 1)
    right = right if right_half == 1 else pltpu.roll(right, CELLS, 1)
    return jnp.where(low_half(left.shape), left, right)


def pack_kernel(fields, forcing, top, bottom, held, edges, sems):
    members = fields.shape[0]
    copies = [pltpu.make_async_copy(fields, held, sems.at[0]), pltpu.make_async_copy(forcing, edges, sems.at[1])]
    for copy in copies:
        copy.start()
    for copy in copies:
        copy.wait()
    for out, start in ((bottom, STEPS), (top, 0)):
        for row in range(STEPS):
            out[pl.ds(row * members, members), :] = held[:, start + row, :]
        edge = edges[pl.ds(start, STEPS), :]
        out[pl.ds(STEPS * members, 2 * STEPS), :] = jnp.concatenate([edge, edge], axis=0)


def observe_kernel(scalars, cells, values, variances, out):
    slots = values.shape[2]
    live = lax.broadcasted_iota(jnp.int32, (1, slots), 1) < scalars[1]
    weight = jnp.where(live, 1.0 / variances[0], 0.0)
    scaled = weight * values[0]
    mine = cells[0, pl.ds(scalars[0], 1), :]
    cell = lax.broadcasted_iota(jnp.int32, (2 * CELLS, slots), 0) % CELLS
    hit = jnp.where(cell == mine, 1.0, 0.0)
    row = lax.broadcasted_iota(jnp.int32, (8, slots), 0)
    terms = jnp.where(row == 0, weight, jnp.where(row == 1, scaled, 0.0))
    sums = lax.dot_general(
        terms, hit, (((1,), (1,)), ((), ())), precision=HIGHEST, preferred_element_type=jnp.float32
    )
    both = jnp.where(low_half((1, LANES)), sums[0:1], sums[1:2])
    out[...] = jnp.broadcast_to(both, (8, LANES))


def step_rows(rows, places, forces, strip, last_strip):
    updated = {}
    for place in places:
        here = rows[place]
        eastern = pltpu.roll(here, here.shape[1] - 1, 1)
        western = pltpu.roll(here, 1, 1)
        far_west = pltpu.roll(here, 2, 1)
        tendency = (
            (eastern - far_west) * western
            - here
            + forces(place)
            + LAT_MIXING * (rows[place - 1] + rows[place + 1] - 2.0 * here)
        )
        value = here + TIME_STEP * tendency
        if place < STEPS:
            value = jnp.where(strip == 0, 0.0, value)
        if place >= 3 * STEPS:
            value = jnp.where(strip == last_strip, 0.0, value)
        updated[place] = value
    return updated


def spread_patches(out, lanes_at, tile, rows):
    for near in range(NEAR):
        block = near % 4
        lanes = slice(block // 2 * LANES, block // 2 * LANES + LANES)
        first, second = rows[near // 4][:, lanes], rows[2 + near // 4][:, lanes]
        joined = halves(first, block % 2, second, block % 2)
        out[near, pl.ds(tile * 8, 8), pl.ds(lanes_at, LANES)] = joined


def early_kernel(last_strip, scalars, before, top, bottom, out, kept):
    members = out.shape[1]
    strip = scalars[2]
    sources = [before, top, bottom]

    def forces(place):
        return sources[place // STEPS][pl.ds(STEPS * members + place % STEPS, 1), :]

    for tile in range(members // 8):
        rows = {
            place: sources[place // STEPS][pl.ds((place % STEPS) * members + tile * 8, 8), :]
            for place in range(3 * STEPS)
        }
        for step in range(STEPS):
            rows = step_rows(rows, range(1 + step, 11 - step), forces, strip, last_strip)
            if step < STEPS - 1:
                for place in range(2):
                    kept[2 * step + place, pl.ds(tile * 8, 8), :] = rows[9 - step + place]
        spread_patches(out, 0, tile, [rows[place] for place in range(4, 8)])


def late_kernel(last_strip, scalars, bottom, after, kept, early, out):
    members = out.shape[1]
    strip = scalars[2]
    sources = [None, None, bottom, after]

    def forces(place):
        return sources[place // STEPS][pl.ds(STEPS * members + place % STEPS, 1), :]

    out[:, :, pl.ds(0, LANES)] = early[...]
    for tile in range(members // 8):
        rows = {
            place: sources[place // STEPS][pl.ds((place % STEPS) * members + tile * 8, 8), :]
            for place in range(10, 16)
        }
        for step in range(STEPS):
            if step > 0:
                for place in range(2):
                    rows[10 - step + place] = kept[2 * step - 2 + place, pl.ds(tile * 8, 8), :]
            rows = step_rows(rows, range(11 - step, 15 - step), forces, strip, last_strip)
        spread_patches(out, LANES, tile, [rows[place] for place in range(8, 12)])


def fold(square):
    return jnp.where(low_half((CELLS, LANES)), square[:CELLS], square[CELLS:])


def unfold(pair):
    low = low_half(pair.shape)
    return jnp.concatenate([jnp.where(low, pair, 0.0), jnp.where(low, 0.0, pair)], axis=0)


def places(shape):
    row = lax.broadcasted_iota(jnp.int32, shape, 0)
    return row, lax.broadcasted_iota(jnp.int32, shape, 1) % CELLS


def pack_symmetric(pair):
    side = CELLS // 2
    row, lane = places((side, LANES))
    take_upper = (lane >= side) & (row > lane - side)
    packed = jnp.where(take_upper, pltpu.roll(pair[:side], side, 1), pair[side:])
    return packed, jnp.sum(jnp.where(row == lane, pair[:side], 0.0), axis=0, keepdims=True)


def unpack_symmetric(packed, diagonals):
    side = CELLS // 2
    across = [halves(packed[0], half, packed[1], half) for half in range(2)]
    stacked = []
    for block in across:
        stacked += [pltpu.roll(block, LANES - side, 1), block]
    turned = jnp.concatenate(stacked, axis=0).T
    row, lane = places((CELLS, LANES))
    direct = ((lane < side) & (row > lane)) | ((lane >= side) & (row >= side) & (row <= lane))
    pairs = []
    for half in range(2):
        straight = jnp.concatenate([pltpu.roll(packed[half], LANES - side, 1), packed[half]], axis=0)
        full = jnp.where(direct, straight, turned[half * CELLS:(half + 1) * CELLS])
        pairs.append(jnp.where((row == lane) & (row < side), diagonals[half], full))
    return pairs


def moments_kernel(states, observed, out):
    lines = []
    for half in range(2):
        block = states[:, pl.ds(half * LANES, LANES)]
        mean = jnp.sum(block, axis=0, keepdims=True) / block.shape[0]
        centred = block - mean
        square = lax.dot_general(
            centred, centred, (((0,), (0,)), ((), ())), precision=HIGHEST, preferred_element_type=jnp.float32
        )
        packed, diagonal = pack_symmetric(fold(square))
        for hi in range(FAR):
            out[hi, pl.ds(half * CELLS // 2, CELLS // 2), :] = packed
        lines += [mean, diagonal]
    row = lax.broadcasted_iota(jnp.int32, (8, LANES), 0)
    tail = observed[...]
    for place, line in enumerate(lines):
        tail = jnp.where(row == place, line, tail)
    for hi in range(FAR):
        out[hi, pl.ds(CELLS, 8), :] = tail


def invert(pairs):
    row, lane = places((8, LANES))
    base = jnp.where(low_half((8, LANES)), 0, CELLS)

    def spread(block, line):
        return jnp.broadcast_to(block[line:line + 1, :], (8, LANES))

    for tile in range(8):
        inside = lane // 8 == tile
        identity = jnp.where(lane == row + 8 * tile, 1.0, 0.0)
        columns = [
            [
                [
                    jnp.take_along_axis(part, base + (8 * tile + c), axis=1, mode="promise_in_bounds")
                    for c in range(8)
                ]
                for part in pair
            ]
            for pair in pairs
        ]
        inverses = [list(factors[tile]) for factors in columns]
        for line in range(8):
            for inverse in inverses:
                reciprocal = 1.0 / spread(inverse[line], line)
                for c in range(8):
                    if c != line:
                        lead = spread(inverse[c], line) * reciprocal
                        inverse[c] = jnp.where(row == line, lead, inverse[c] - inverse[line] * lead)
                inverse[line] = jnp.where(row == line, reciprocal, -inverse[line] * reciprocal)
        for pair, factors, inverse in zip(pairs, columns, inverses):
            block = jnp.where(inside, identity, pair[tile])
            lead = inverse[0] * spread(block, 0)
            for c in range(1, 8):
                lead = lead + inverse[c] * spread(block, c)
            pair[tile] = lead
            leads = [spread(lead, c) for c in range(8)]
            for place in range(8):
                if place != tile:
                    rest = jnp.where(inside, 0.0, pair[place])
                    for c in range(8):
                        rest = rest - factors[place][c] * leads[c]
                    pair[place] = rest


def analyse_kernel(received, states, out):
    group = states.shape[0]
    members = FAR * group
    side = CELLS // 2

    def line(hi, place):
        return received[hi, pl.ds(CELLS + place, 1), :]

    def total(part):
        return part(0) + part(1) + part(2) + part(3)

    packed = [total(lambda hi: received[hi, pl.ds(half * side, side), :]) for half in range(2)]
    within = unpack_symmetric(packed, [total(lambda hi: line(hi, 2 * half + 1)) for half in range(2)])
    row, lane = places((CELLS, LANES))
    identity = jnp.where(row == lane, 1.0, 0.0)
    means, weights, shifts, pairs = [], [], [], []
    for half in range(2):
        mean = total(lambda hi: line(hi, 2 * half)) / FAR
        which = lax.broadcasted_iota(jnp.int32, (8, LANES), 0)
        offsets = jnp.zeros((8, LANES), jnp.float32)
        for hi in range(FAR):
            offsets = jnp.where(which == hi, line(hi, 2 * half) - mean, offsets)
        between = lax.dot_general(
            offsets, offsets, (((0,), (0,)), ((), ())), precision=HIGHEST, preferred_element_type=jnp.float32
        )
        covariance = (within[half] + group * fold(between)) / (members - 1)
        first, second = line(2 * half, 4), line(2 * half + 1, 4)
        weight = halves(first, 0, second, 0)
        shift = halves(first, 1, second, 1) - weight * mean
        shift = jnp.dot(
            jnp.broadcast_to(shift, (8, LANES)),
            unfold(covariance),
            precision=HIGHEST,
            preferred_element_type=jnp.float32,
        )
        system = covariance * weight + identity
        means.append(mean)
        shifts.append(shift[:1])
        pairs.append([system[8 * tile:8 * tile + 8] for tile in range(8)])
    invert(pairs)
    for half in range(2):
        block = states[:, pl.ds(half * LANES, LANES)]
        spread = 0.5 * (block - means[half])
        gain = unfold(jnp.concatenate(pairs[half], axis=0))
        out[:, pl.ds(half * LANES, LANES)] = (block - spread) + lax.dot_general(
            spread + shifts[half],
            gain,
            (((1,), (1,)), ((), ())),
            precision=HIGHEST,
            preferred_element_type=jnp.float32,
        )


def unpack_kernel(arrived, out):
    for row in range(out.shape[1]):
        hi, side = divmod(row, 2)
        lanes = pl.ds(hi // 2 * LANES, LANES)
        for pair in range(2):
            near = 4 * side + 2 * pair
            joined = halves(arrived[near, :, lanes], hi % 2, arrived[near + 1, :, lanes], hi % 2)
            out[:, row, pl.ds(pair * LANES, LANES)] = joined


VMEM = pl.BlockSpec(memory_space=pltpu.VMEM)
SMEM = pl.BlockSpec(memory_space=pltpu.SMEM)
HBM = pl.BlockSpec(memory_space=pltpu.HBM)


def call(kernel, outs, in_specs, args, scratch=(), flops=1_000_000):
    many = isinstance(outs, list)
    shapes = [jax.ShapeDtypeStruct(s, jnp.float32) for s in (outs if many else [outs])]
    return pl.pallas_call(
        kernel,
        out_shape=shapes if many else shapes[0],
        in_specs=in_specs,
        out_specs=[VMEM] * len(shapes) if many else VMEM,
        scratch_shapes=list(scratch),
        compiler_params=pltpu.CompilerParams(vmem_limit_bytes=8 * 1024 * 1024),
        cost_estimate=pl.CostEstimate(flops=flops, bytes_accessed=500_000, transcendentals=0),
    )(*args)


def local(fields, forcing, obs_cell, obs_count, obs_value, obs_var):
    members, rows, lon = fields.shape
    strips = lax.axis_size("lat")
    scalars = jnp.stack([lax.axis_index("mem"), obs_count[0, 0], lax.axis_index("lat")]).astype(jnp.int32)
    height = STEPS * members + 2 * STEPS
    top, bottom = call(
        pack_kernel,
        [(height, lon)] * 2,
        [HBM, HBM],
        (fields, forcing),
        [pltpu.VMEM(fields.shape, jnp.float32), pltpu.VMEM(forcing.shape, jnp.float32), pltpu.SemaphoreType.DMA((2,))],
    )
    up = [(i, i + 1) for i in range(strips - 1)]
    down = [(j, i) for i, j in up]
    before = lax.ppermute(bottom, "lat", up)
    after = lax.ppermute(top, "lat", down)
    observed = call(observe_kernel, (8, LANES), [SMEM, VMEM, VMEM, VMEM], (scalars, obs_cell, obs_value, obs_var))
    early, kept = call(
        functools.partial(early_kernel, strips - 1),
        [(NEAR, members, LANES), (6, members, lon)],
        [SMEM, VMEM, VMEM, VMEM],
        (scalars, before, top, bottom),
        flops=10_000_000,
    )
    states = call(
        functools.partial(late_kernel, strips - 1),
        (NEAR, members, lon),
        [SMEM, VMEM, VMEM, VMEM, VMEM],
        (scalars, bottom, after, kept, early),
    )
    states = lax.all_to_all(states, "mem", 0, 0, axis_index_groups=NEAR_GROUPS, tiled=True)
    states = states.reshape(NEAR * members, lon)
    partial = call(moments_kernel, (FAR, CELLS + 8, LANES), [VMEM, VMEM], (states, observed))
    received = lax.all_to_all(partial, "mem", 0, 0, axis_index_groups=FAR_GROUPS, tiled=True)
    result = call(analyse_kernel, states.shape, [VMEM, VMEM], (received, states))
    result = result.reshape(NEAR, members, lon)
    result = lax.all_to_all(result, "mem", 0, 0, axis_index_groups=NEAR_GROUPS, tiled=True)
    return call(unpack_kernel, (members, rows, lon), [VMEM], (result,))


def solution(mesh):
    placed = (
        P("mem", "lat", None),
        P("lat", None),
        P("lat", None, None),
        P("lat", "mem"),
        P("lat", "mem", None),
        P("lat", "mem", None),
    )
    return jax.shard_map(local, mesh=mesh, in_specs=placed, out_specs=P("mem", "lat", None), check_vma=False)
```

time: 86.9 us -> 75 us (0.86)
  Pallas kernels: 15.1 us -> 9.89 us
  blocking collectives: 44.5 us -> 40.1 us
  waiting for transfers between devices: 11.8 us -> 9.94 us
    pallas_call x6 -> x7, Pallas kernels: 15.1 us -> 9.89 us  [call(): pl.pallas_call(kernel, out_shape=shapes if many else shapes[0], in_specs=...]
    all_to_all x1, blocking collectives: 15.5 us -> 12.6 us  [local(): lax.all_to_all(result, 'mem', 0, 0, axis_index_groups=NEAR_GROUPS, tiled=...]
    ppermute x1, waiting for transfers between devices: 6.09 us -> 4.22 us  [local(): after = lax.ppermute(top, 'lat', down)]
    all_to_all x1, blocking collectives: 29 us -> 27.4 us  [local(): lax.all_to_all(partial, 'mem', 0, 0, axis_index_groups=FAR_GROUPS, tiled=...]
  transfers between devices with their start and end apart: 3 -> 3, of which waited for: 2 -> 2; matrix products, arithmetic and copies ran while one was open for 0% -> 0% of each run, Pallas kernels for 1% -> 3%
where the time goes in v2:
time: 75 us; the launch traced here: 74.6 us
  blocking collectives  40.1 us (53%)
  starting transfers between devices  12.3 us (16%)
  waiting for transfers between devices  9.94 us (13%)
  Pallas kernels  9.89 us (13%)
  local copies, waits for them, and re-layouts  1.66 us (2%)
    all_to_all x1, blocking collectives, local(): lax.all_to_all(partial, 'mem', 0, 0, axis_index_groups=FAR_GROUPS, tiled=...  27.4 us
    all_to_all x1, blocking collectives, local(): lax.all_to_all(result, 'mem', 0, 0, axis_index_groups=NEAR_GROUPS, tiled=...  12.6 us
    pallas_call x7, Pallas kernels, call(): pl.pallas_call(kernel, out_shape=shapes if many else shapes[0], in_specs=...  9.89 us
    all_to_all x1, starting transfers between devices, local(): lax.all_to_all(states, 'mem', 0, 0, axis_index_groups=NEAR_GROUPS, tiled=...  6.61 us
    all_to_all x1, waiting for transfers between devices, local(): lax.all_to_all(states, 'mem', 0, 0, axis_index_groups=NEAR_GROUPS, tiled=...  5.71 us
    ppermute x1, starting transfers between devices, local(): before = lax.ppermute(bottom, 'lat', up)  4.37 us
    ppermute x1, waiting for transfers between devices, local(): after = lax.ppermute(top, 'lat', down)  4.22 us
    unnamed x10, local copies, waits for them, and re-layouts  1.66 us
  transfers between devices with their start and end apart: 3, of which 2 were waited for; matrix products, arithmetic and copies ran while one was open for 0% of the time, Pallas kernels for 3%

profile of v2, /device:TPU:1, one launch (start us, length us, event | category | flops | bytes accessed | tf_op | source)
XLA Modules:
  0.0 74.6 jit_solution(13507593351527662550)
XLA Ops:
  0.0 0.0 copy-start
  0.0 0.9 %copy-done = f32[32,8,256]{2,1,0:T(8,128)S(1)} copy-done((f32[32,8,256]{2,1,0:T(8,128)S(1)}, f32[32,8,256]{2,1,0:T(8,128)}, u32[]{:S(2)}) %copy-start) | copy-done | bytes 262168
  1.0 0.0 copy-start.2
  1.0 0.7 copy-done.2
  1.6 0.1 shard_map.64
  1.8 4.4 %collective-permute-start.1 = (f32[136,256]{1,0:T(8,128)S(1)}, f32[136,256]{1,0:T(8,128)S(1)}, u32[]{:S(2)}, u32[]{:S(2)}) collective-permute-start(f32[136,256]{1,0:T(8,128)S(1)} %get-tuple-element.9.bottom), channel_id=1, source_target_pairs={{0,1},{1,2},{2,3},{3,4},{4,5},{5,6},{6,7},{7,8},{8,9},{9,10},{10,1... | collective-permute-start | bytes 417800 | tf_op jit(solution)/shard_map/ppermute | solution.py:337
  6.2 1.3 %collective-permute-start = (f32[136,256]{1,0:T(8,128)S(1)}, f32[136,256]{1,0:T(8,128)S(1)}, u32[]{:S(2)}, u32[]{:S(2)}) collective-permute-start(f32[136,256]{1,0:T(8,128)S(1)} %get-tuple-element.10.top), channel_id=1, source_target_pairs={{1,0},{2,1},{3,2},{4,3},{5,4},{6,5},{7,6},{8,7},{9,8},{10,9},{11,1... | collective-permute-start | bytes 417800 | tf_op jit(solution)/shard_map/ppermute | solution.py:338
  8.1 0.1 pad_add_fusion.scalars
  8.2 0.0 collective-permute-done.1.before
  8.2 1.9 %shard_map.65 = (f32[8,32,128]{2,1,0:T(8,128)S(1)}, f32[6,32,256]{2,1,0:T(8,128)S(1)}) custom-call(s32[3]{0:T(128)S(1)} %pad_add_fusion.scalars, f32[136,256]{1,0:T(8,128)S(1)} %collective-permute-done.1.before, f32[136,256]{1,0:T(8,128)S(1)} %get-tuple-element.10.top, f32[136,256]{1,0:T(8,128)S(1)} %get-tuple-element.9.bottom), custom_call_target="tpu_custom_call" | custom-call | flops 10000000 | bytes 500000 | tf_op jit(solution)/shard_map/pallas_call | solution.py:312
  10.1 4.2 %collective-permute-done.after = f32[136,256]{1,0:T(8,128)S(1)} collective-permute-done((f32[136,256]{1,0:T(8,128)S(1)}, f32[136,256]{1,0:T(8,128)S(1)}, u32[]{:S(2)}, u32[]{:S(2)}) %collective-permute-start) | collective-permute-done | bytes 139296 | tf_op jit(solution)/shard_map/ppermute | solution.py:338
  14.3 2.1 %shard_map.66 = f32[8,32,256]{2,1,0:T(8,128)} custom-call(s32[3]{0:T(128)S(1)} %pad_add_fusion.scalars, f32[136,256]{1,0:T(8,128)S(1)} %get-tuple-element.9.bottom, f32[136,256]{1,0:T(8,128)S(1)} %collective-permute-done.after, f32[6,32,256]{2,1,0:T(8,128)S(1)} %get-tuple-element.11.kept, f32[8,32,128]{2,1,0:T(8,128)S(1)} %get-tuple-element.12.early), custom_call_target="tpu_custom_call" | custom-call | flops 1000000 | bytes 500000 | tf_op jit(solution)/shard_map/pallas_call | solution.py:312
  16.4 0.0 copy-start.3
  16.4 6.6 %all-to-all-start = ((f32[8,32,256]{2,1,0:T(8,128)}), f32[8,32,256]{2,1,0:T(8,128)S(1)}, u32[]{:S(2)}, u32[]{:S(2)}) async-start(f32[8,32,256]{2,1,0:T(8,128)} %shard_map.66), calls=%async_computation | async-start | bytes 524288 | tf_op jit(solution)/shard_map/all_to_all | solution.py:353
  23.0 0.0 copy-done.1
  23.0 0.0 copy-done.3
  23.0 0.0 copy-done.4
  23.0 0.7 shard_map.67.observed
  23.7 5.7 %all-to-all-done = f32[8,32,256]{2,1,0:T(8,128)S(1)} async-done(((f32[8,32,256]{2,1,0:T(8,128)}), f32[8,32,256]{2,1,0:T(8,128)S(1)}, u32[]{:S(2)}, u32[]{:S(2)}) %all-to-all-start) | async-done | bytes 262176 | tf_op jit(solution)/shard_map/all_to_all | solution.py:353
  29.5 0.5 shard_map.68
  30.0 27.4 %all_to_all.15.received = f32[4,72,128]{2,1,0:T(8,128)S(1)} all-to-all(f32[4,72,128]{2,1,0:T(8,128)S(1)} %shard_map.68), channel_id=1, replica_groups={{0,128,256,384},{16,144,272,400},{32,160,288,416},{48,176,304,432},{64,..., dimensions={0} | all-to-all | bytes 294912 | tf_op jit(solution)/shard_map/all_to_all | solution.py:356
  57.4 3.6 %shard_map.69 = f32[256,256]{1,0:T(8,128)S(1)} custom-call(f32[4,72,128]{2,1,0:T(8,128)S(1)} %all_to_all.15.received, f32[256,256]{1,0:T(8,128)S(1)} %bitcast.7), custom_call_target="tpu_custom_call" | custom-call | flops 1000000 | bytes 500000 | tf_op jit(solution)/shard_map/pallas_call | solution.py:312
  61.0 12.6 %all_to_all.16.arrived = f32[8,32,256]{2,1,0:T(8,128)S(1)} all-to-all(f32[8,32,256]{2,1,0:T(8,128)S(1)} %bitcast.8), channel_id=1, replica_groups={{0,16,32,48,64,80,96,112},{128,144,160,176,192,208,224,240},{256,272,28..., dimensions={0} | all-to-all | bytes 524288 | tf_op jit(solution)/shard_map/all_to_all | solution.py:359
  73.7 0.9 %shard_map.70 = f32[32,8,256]{2,1,0:T(8,128)} custom-call(f32[8,32,256]{2,1,0:T(8,128)S(1)} %all_to_all.16.arrived), custom_call_target="tpu_custom_call" | custom-call | flops 1000000 | bytes 500000 | tf_op jit(solution)/shard_map/pallas_call | solution.py:312
  (2 shorter events, 0.0 us)
Async XLA Ops:
  0.0 0.9 %copy-start = (f32[32,8,256]{2,1,0:T(8,128)S(1)}, f32[32,8,256]{2,1,0:T(8,128)}, u32[]{:S(2)}) copy-start(f32[32,8,256]{2,1,0:T(8,128)} %fields.1) | copy-start | bytes 786436
  1.0 0.7 copy-start.2
  1.8 6.4 %collective-permute-start.1 = (f32[136,256]{1,0:T(8,128)S(1)}, f32[136,256]{1,0:T(8,128)S(1)}, u32[]{:S(2)}, u32[]{:S(2)}) collective-permute-start(f32[136,256]{1,0:T(8,128)S(1)} %get-tuple-element.9.bottom), channel_id=1, source_target_pairs={{0,1},{1,2},{2,3},{3,4},{4,5},{5,6},{6,7},{7,8},{8,9},{9,10},{10,1... | collective-permute-start | bytes 417800 | tf_op jit(solution)/shard_map/ppermute | solution.py:337
  6.2 8.1 %collective-permute-start = (f32[136,256]{1,0:T(8,128)S(1)}, f32[136,256]{1,0:T(8,128)S(1)}, u32[]{:S(2)}, u32[]{:S(2)}) collective-permute-start(f32[136,256]{1,0:T(8,128)S(1)} %get-tuple-element.10.top), channel_id=1, source_target_pairs={{1,0},{2,1},{3,2},{4,3},{5,4},{6,5},{7,6},{8,7},{9,8},{10,9},{11,1... | collective-permute-start | bytes 417800 | tf_op jit(solution)/shard_map/ppermute | solution.py:338
  16.4 6.6 %copy-start.1 = (s32[1,32,256]{2,1,0:T(8,128)S(1)}, s32[1,32,256]{2,1,0:T(8,128)}, u32[]{:S(2)}) copy-start(s32[1,32,256]{2,1,0:T(8,128)} %cells.1) | copy-start | bytes 98308
  16.4 6.6 %copy-start.3 = (f32[1,1,256]{2,1,0:T(1,128)S(1)}, f32[1,1,256]{2,1,0:T(1,128)}, u32[]{:S(2)}) copy-start(f32[1,1,256]{2,1,0:T(1,128)} %values.1) | copy-start | bytes 3076
  16.4 6.6 %copy-start.4 = (f32[1,1,256]{2,1,0:T(1,128)S(1)}, f32[1,1,256]{2,1,0:T(1,128)}, u32[]{:S(2)}) copy-start(f32[1,1,256]{2,1,0:T(1,128)} %variances.1) | copy-start | bytes 3076
  16.4 13.1 %all-to-all-start = ((f32[8,32,256]{2,1,0:T(8,128)}), f32[8,32,256]{2,1,0:T(8,128)S(1)}, u32[]{:S(2)}, u32[]{:S(2)}) async-start(f32[8,32,256]{2,1,0:T(8,128)} %shard_map.66), calls=%async_computation | async-start | bytes 524288 | tf_op jit(solution)/shard_map/all_to_all | solution.py:353

commit v3 on v2

--- a/solution.py
+++ b/solution.py
@@ -16,7 +16,6 @@
 HIGHEST = lax.Precision.HIGHEST
 LANES = 128
 NEAR_GROUPS = [[hi * NEAR + near for near in range(NEAR)] for hi in range(FAR)]
-FAR_GROUPS = [[hi * NEAR + near for hi in range(FAR)] for near in range(NEAR)]
 
 
 def low_half(shape):
@@ -43,7 +42,7 @@
         out[pl.ds(STEPS * members, 2 * STEPS), :] = jnp.concatenate([edge, edge], axis=0)
 
 
-def observe_kernel(scalars, cells, values, variances, out):
+def observe(scalars, cells, values, variances, out):
     slots = values.shape[2]
     live = lax.broadcasted_iota(jnp.int32, (1, slots), 1) < scalars[1]
     weight = jnp.where(live, 1.0 / variances[0], 0.0)
@@ -88,10 +87,11 @@
         lanes = slice(block // 2 * LANES, block // 2 * LANES + LANES)
         first, second = rows[near // 4][:, lanes], rows[2 + near // 4][:, lanes]
         joined = halves(first, block % 2, second, block % 2)
-        out[near, pl.ds(tile * 8, 8), pl.ds(lanes_at, LANES)] = joined
-
-
-def early_kernel(last_strip, scalars, before, top, bottom, out, kept):
+        out[near, pl.ds(tile * first.shape[0], first.shape[0]), pl.ds(lanes_at, LANES)] = joined
+
+
+def early_kernel(last_strip, scalars, cells, values, variances, before, top, bottom, out, kept, observed):
+    observe(scalars, cells, values, variances, observed)
     members = out.shape[1]
     strip = scalars[2]
     sources = [before, top, bottom]
@@ -99,16 +99,16 @@
     def forces(place):
         return sources[place // STEPS][pl.ds(STEPS * members + place % STEPS, 1), :]
 
-    for tile in range(members // 8):
+    for tile in range(members // 32):
         rows = {
-            place: sources[place // STEPS][pl.ds((place % STEPS) * members + tile * 8, 8), :]
+            place: sources[place // STEPS][pl.ds((place % STEPS) * members + tile * 32, 32), :]
             for place in range(3 * STEPS)
         }
         for step in range(STEPS):
             rows = step_rows(rows, range(1 + step, 11 - step), forces, strip, last_strip)
             if step < STEPS - 1:
                 for place in range(2):
-                    kept[2 * step + place, pl.ds(tile * 8, 8), :] = rows[9 - step + place]
+                    kept[2 * step + place, pl.ds(tile * 32, 32), :] = rows[9 - step + place]
         spread_patches(out, 0, tile, [rows[place] for place in range(4, 8)])
 
 
@@ -121,15 +121,15 @@
         return sources[place // STEPS][pl.ds(STEPS * members + place % STEPS, 1), :]
 
     out[:, :, pl.ds(0, LANES)] = early[...]
-    for tile in range(members // 8):
+    for tile in range(members // 32):
         rows = {
-            place: sources[place // STEPS][pl.ds((place % STEPS) * members + tile * 8, 8), :]
+            place: sources[place // STEPS][pl.ds((place % STEPS) * members + tile * 32, 32), :]
             for place in range(10, 16)
         }
         for step in range(STEPS):
             if step > 0:
                 for place in range(2):
-                    rows[10 - step + place] = kept[2 * step - 2 + place, pl.ds(tile * 8, 8), :]
+                    rows[10 - step + place] = kept[2 * step - 2 + place, pl.ds(tile * 32, 32), :]
             rows = step_rows(rows, range(11 - step, 15 - step), forces, strip, last_strip)
         spread_patches(out, LANES, tile, [rows[place] for place in range(8, 12)])
 
@@ -183,15 +183,13 @@
             centred, centred, (((0,), (0,)), ((), ())), precision=HIGHEST, preferred_element_type=jnp.float32
         )
         packed, diagonal = pack_symmetric(fold(square))
-        for hi in range(FAR):
-            out[hi, pl.ds(half * CELLS // 2, CELLS // 2), :] = packed
+        out[pl.ds(half * CELLS // 2, CELLS // 2), :] = packed
         lines += [mean, diagonal]
     row = lax.broadcasted_iota(jnp.int32, (8, LANES), 0)
     tail = observed[...]
     for place, line in enumerate(lines):
         tail = jnp.where(row == place, line, tail)
-    for hi in range(FAR):
-        out[hi, pl.ds(CELLS, 8), :] = tail
+    out[pl.ds(CELLS, 8), :] = tail
 
 
 def invert(pairs):
@@ -204,13 +202,16 @@
     for tile in range(8):
         inside = lane // 8 == tile
         identity = jnp.where(lane == row + 8 * tile, 1.0, 0.0)
+        near = (tile, (tile + 1) % 8)
         columns = [
             [
                 [
                     jnp.take_along_axis(part, base + (8 * tile + c), axis=1, mode="promise_in_bounds")
                     for c in range(8)
                 ]
-                for part in pair
+                if place in near
+                else None
+                for place, part in enumerate(pair)
             ]
             for pair in pairs
         ]
@@ -228,9 +229,22 @@
             lead = inverse[0] * spread(block, 0)
             for c in range(1, 8):
                 lead = lead + inverse[c] * spread(block, c)
+            whole = jnp.concatenate(pair, axis=0)
+            across = jnp.where(places((CELLS, LANES))[1] // 8 == tile, whole, 0.0)
+            low = low_half((8, LANES))
+            empty = jnp.zeros((8, LANES), jnp.float32)
+            rows = [empty] * 16
+            rows[tile] = jnp.where(low, lead, 0.0)
+            rows[8 + tile] = jnp.where(low, 0.0, lead)
+            product = jnp.dot(
+                across, jnp.concatenate(rows, axis=0), precision=HIGHEST, preferred_element_type=jnp.float32
+            )
+            for place in range(8):
+                if place not in near:
+                    pair[place] = jnp.where(inside, 0.0, pair[place]) - product[8 * place:8 * place + 8]
             pair[tile] = lead
             leads = [spread(lead, c) for c in range(8)]
-            for place in range(8):
+            for place in near:
                 if place != tile:
                     rest = jnp.where(inside, 0.0, pair[place])
                     for c in range(8):
@@ -238,18 +252,26 @@
                     pair[place] = rest
 
 
-def analyse_kernel(received, states, out):
+def analyse_kernel(scalars, own, ahead1, ahead2, ahead3, states, out):
     group = states.shape[0]
     members = FAR * group
     side = CELLS // 2
-
-    def line(hi, place):
-        return received[hi, pl.ds(CELLS + place, 1), :]
+    received = (own, ahead1, ahead2, ahead3)
+
+    def line(back, place):
+        return received[back][pl.ds(CELLS + place, 1), :]
+
+    def observed(hi):
+        back = (scalars[0] // NEAR + FAR - hi) % FAR
+        value = line(0, 4)
+        for place in range(1, FAR):
+            value = jnp.where(back == place, line(place, 4), value)
+        return value
 
     def total(part):
         return part(0) + part(1) + part(2) + part(3)
 
-    packed = [total(lambda hi: received[hi, pl.ds(half * side, side), :]) for half in range(2)]
+    packed = [total(lambda back: received[back][pl.ds(half * side, side), :]) for half in range(2)]
     within = unpack_symmetric(packed, [total(lambda hi: line(hi, 2 * half + 1)) for half in range(2)])
     row, lane = places((CELLS, LANES))
     identity = jnp.where(row == lane, 1.0, 0.0)
@@ -264,7 +286,7 @@
             offsets, offsets, (((0,), (0,)), ((), ())), precision=HIGHEST, preferred_element_type=jnp.float32
         )
         covariance = (within[half] + group * fold(between)) / (members - 1)
-        first, second = line(2 * half, 4), line(2 * half + 1, 4)
+        first, second = observed(2 * half), observed(2 * half + 1)
         weight = halves(first, 0, second, 0)
         shift = halves(first, 1, second, 1) - weight * mean
         shift = jnp.dot(
@@ -325,6 +347,7 @@
     strips = lax.axis_size("lat")
     scalars = jnp.stack([lax.axis_index("mem"), obs_count[0, 0], lax.axis_index("lat")]).astype(jnp.int32)
     height = STEPS * members + 2 * STEPS
+    fields, forcing = (pltpu.with_memory_space_constraint(value, pltpu.HBM) for value in (fields, forcing))
     top, bottom = call(
         pack_kernel,
         [(height, lon)] * 2,
@@ -336,12 +359,11 @@
     down = [(j, i) for i, j in up]
     before = lax.ppermute(bottom, "lat", up)
     after = lax.ppermute(top, "lat", down)
-    observed = call(observe_kernel, (8, LANES), [SMEM, VMEM, VMEM, VMEM], (scalars, obs_cell, obs_value, obs_var))
-    early, kept = call(
+    early, kept, observed = call(
         functools.partial(early_kernel, strips - 1),
-        [(NEAR, members, LANES), (6, members, lon)],
-        [SMEM, VMEM, VMEM, VMEM],
-        (scalars, before, top, bottom),
+        [(NEAR, members, LANES), (6, members, lon), (8, LANES)],
+        [SMEM] + [VMEM] * 6,
+        (scalars, obs_cell, obs_value, obs_var, before, top, bottom),
         flops=10_000_000,
     )
     states = call(
@@ -352,9 +374,18 @@
     )
     states = lax.all_to_all(states, "mem", 0, 0, axis_index_groups=NEAR_GROUPS, tiled=True)
     states = states.reshape(NEAR * members, lon)
-    partial = call(moments_kernel, (FAR, CELLS + 8, LANES), [VMEM, VMEM], (states, observed))
-    received = lax.all_to_all(partial, "mem", 0, 0, axis_index_groups=FAR_GROUPS, tiled=True)
-    result = call(analyse_kernel, states.shape, [VMEM, VMEM], (received, states))
+    partial = call(moments_kernel, (CELLS + 8, LANES), [VMEM, VMEM], (states, observed))
+    size = FAR * NEAR
+    onward = [(i, (i + NEAR) % size) for i in range(size)]
+    ahead1 = lax.ppermute(partial, "mem", onward)
+    ahead3 = lax.ppermute(partial, "mem", [(j, i) for i, j in onward])
+    ahead2 = lax.ppermute(ahead1, "mem", onward)
+    result = call(
+        analyse_kernel,
+        states.shape,
+        [SMEM] + [VMEM] * (FAR + 1),
+        (scalars, partial, ahead1, ahead2, ahead3, states),
+    )
     result = result.reshape(NEAR, members, lon)
     result = lax.all_to_all(result, "mem", 0, 0, axis_index_groups=NEAR_GROUPS, tiled=True)
     return call(unpack_kernel, (members, rows, lon), [VMEM], (result,))

time: 75 us -> 67.6 us (0.901)
  blocking collectives: 40.1 us -> 24.3 us
  starting transfers between devices: 12.3 us -> 25 us
  waiting for transfers between devices: 9.94 us -> 7.43 us
  Pallas kernels: 9.89 us -> 8.69 us
  local copies, waits for them, and re-layouts: 1.66 us -> 0.6 us
    ppermute x0 -> x3, starting transfers between devices: none -> 19.3 us  [the longest x1 8.81 us: local(): ahead1 = lax.ppermute(partial, 'mem', onward)]
    all_to_all x1, blocking collectives: 27.4 us -> 12.7 us  [local(): lax.all_to_all(states, 'mem', 0, 0, axis_index_groups=NEAR_GROUPS, tiled=...]
    all_to_all x1 -> x0, starting transfers between devices: 6.61 us -> none  [local(): lax.all_to_all(states, 'mem', 0, 0, axis_index_groups=NEAR_GROUPS, tiled=...]
    all_to_all x1 -> x0, waiting for transfers between devices: 5.71 us -> none  [local(): lax.all_to_all(states, 'mem', 0, 0, axis_index_groups=NEAR_GROUPS, tiled=...]
    ppermute x0 -> x3, waiting for transfers between devices: none -> 3.43 us  [the longest x1 3.14 us: local(): ahead2 = lax.ppermute(ahead1, 'mem', onward)]
    pallas_call x7 -> x6, Pallas kernels: 9.89 us -> 8.69 us  [call(): pl.pallas_call(kernel, out_shape=shapes if many else shapes[0], in_specs=...]
    all_to_all x1, blocking collectives: 12.6 us -> 11.6 us  [local(): lax.all_to_all(result, 'mem', 0, 0, axis_index_groups=NEAR_GROUPS, tiled=...]
    unnamed x10 -> x6, local copies, waits for them, and re-layouts: 1.66 us -> 0.6 us
  transfers between devices with their start and end apart: 3 -> 5, of which waited for: 2 -> 3; matrix products, arithmetic and copies ran while one was open for 0% -> 0% of each run, Pallas kernels for 3% -> 2%
where the time goes in v3:
time: 67.6 us; the launch traced here: 66.8 us
  starting transfers between devices  25 us (37%)
  blocking collectives  24.3 us (36%)
  Pallas kernels  8.69 us (13%)
  waiting for transfers between devices  7.43 us (11%)
  between operations  0.75 us (1%)
    all_to_all x1, blocking collectives, local(): lax.all_to_all(states, 'mem', 0, 0, axis_index_groups=NEAR_GROUPS, tiled=...  12.7 us
    all_to_all x1, blocking collectives, local(): lax.all_to_all(result, 'mem', 0, 0, axis_index_groups=NEAR_GROUPS, tiled=...  11.6 us
    ppermute x1, starting transfers between devices, local(): ahead1 = lax.ppermute(partial, 'mem', onward)  8.81 us
    pallas_call x6, Pallas kernels, call(): pl.pallas_call(kernel, out_shape=shapes if many else shapes[0], in_specs=...  8.69 us
    ppermute x1, starting transfers between devices, local(): ahead3 = lax.ppermute(partial, 'mem', [(j, i) for i, j in onward])  5.33 us
    ppermute x1, starting transfers between devices, local(): ahead2 = lax.ppermute(ahead1, 'mem', onward)  5.18 us
    ppermute x1, starting transfers between devices, local(): before = lax.ppermute(bottom, 'lat', up)  4.37 us
    ppermute x1, waiting for transfers between devices, local(): after = lax.ppermute(top, 'lat', down)  4.01 us
  transfers between devices with their start and end apart: 5, of which 3 were waited for; matrix products, arithmetic and copies ran while one was open for 0% of the time, Pallas kernels for 2%

profile of v3, /device:TPU:1, one launch (start us, length us, event | category | flops | bytes accessed | tf_op | source)
XLA Modules:
  0.0 66.8 jit_solution(11818679022598527432)
XLA Ops:
  0.0 1.1 %shard_map.64 = (f32[136,256]{1,0:T(8,128)S(1)}, f32[136,256]{1,0:T(8,128)S(1)}) custom-call(f32[32,8,256]{2,1,0:T(8,128)} %fields.1, f32[8,256]{1,0:T(8,128)} %forcing.1), custom_call_target="tpu_custom_call" | custom-call | flops 1000000 | bytes 500000 | tf_op jit(solution)/shard_map/pallas_call | solution.py:334
  1.1 4.4 %collective-permute-start.1 = (f32[136,256]{1,0:T(8,128)S(1)}, f32[136,256]{1,0:T(8,128)S(1)}, u32[]{:S(2)}, u32[]{:S(2)}) collective-permute-start(f32[136,256]{1,0:T(8,128)S(1)} %get-tuple-element.10.bottom), channel_id=1, source_target_pairs={{0,1},{1,2},{2,3},{3,4},{4,5},{5,6},{6,7},{7,8},{8,9},{9,10},{10,1... | collective-permute-start | bytes 417800 | tf_op jit(solution)/shard_map/ppermute | solution.py:360
  5.4 1.3 %collective-permute-start = (f32[136,256]{1,0:T(8,128)S(1)}, f32[136,256]{1,0:T(8,128)S(1)}, u32[]{:S(2)}, u32[]{:S(2)}) collective-permute-start(f32[136,256]{1,0:T(8,128)S(1)} %get-tuple-element.11.top), channel_id=1, source_target_pairs={{1,0},{2,1},{3,2},{4,3},{5,4},{6,5},{7,6},{8,7},{9,8},{10,9},{11,1... | collective-permute-start | bytes 417800 | tf_op jit(solution)/shard_map/ppermute | solution.py:361
  7.4 0.0 copy-start.1
  7.4 0.0 copy-start.2
  7.4 0.1 pad_add_fusion.scalars
  7.5 0.0 collective-permute-done.1.before
  7.5 0.0 copy-done
  7.5 0.6 copy-done.1
  8.1 0.0 copy-done.2
  8.1 1.5 %shard_map.65 = (f32[8,32,128]{2,1,0:T(8,128)S(1)}, f32[6,32,256]{2,1,0:T(8,128)S(1)}, f32[8,128]{1,0:T(8,128)S(1)}) custom-call(s32[3]{0:T(128)S(1)} %pad_add_fusion.scalars, s32[1,32,256]{2,1,0:T(8,128)S(1)} %copy-done, f32[1,1,256]{2,1,0:T(1,128)S(1)} %copy-done.1, f32[1,1,256]{2,1,0:T(1,128)S(1)} %copy-done.2, ...), custom_call_target="tpu_custom_call" | custom-call | flops 10000000 | bytes 500000 | tf_op jit(solution)/shard_map/pallas_call | solution.py:334
  9.6 4.0 %collective-permute-done.after = f32[136,256]{1,0:T(8,128)S(1)} collective-permute-done((f32[136,256]{1,0:T(8,128)S(1)}, f32[136,256]{1,0:T(8,128)S(1)}, u32[]{:S(2)}, u32[]{:S(2)}) %collective-permute-start) | collective-permute-done | bytes 139296 | tf_op jit(solution)/shard_map/ppermute | solution.py:361
  13.6 1.1 %shard_map.66 = f32[8,32,256]{2,1,0:T(8,128)S(1)} custom-call(s32[3]{0:T(128)S(1)} %pad_add_fusion.scalars, f32[136,256]{1,0:T(8,128)S(1)} %get-tuple-element.10.bottom, f32[136,256]{1,0:T(8,128)S(1)} %collective-permute-done.after, f32[6,32,256]{2,1,0:T(8,128)S(1)} %get-tuple-element.12.kept, f32[8,32,128]{2,1,0:T(8,128)S(1)} %get-tuple-element.13.early), custom_call_target="tpu_custom_call" | custom-call | flops 1000000 | bytes 500000 | tf_op jit(solution)/shard_map/pallas_call | solution.py:334
  14.7 12.7 %all_to_all.10 = f32[8,32,256]{2,1,0:T(8,128)S(1)} all-to-all(f32[8,32,256]{2,1,0:T(8,128)S(1)} %shard_map.66), channel_id=1, replica_groups={{0,16,32,48,64,80,96,112},{128,144,160,176,192,208,224,240},{256,272,28..., dimensions={0} | all-to-all | bytes 524288 | tf_op jit(solution)/shard_map/all_to_all | solution.py:375
  27.4 0.5 shard_map.67.own
  28.0 8.8 %collective-permute-start.2 = (f32[72,128]{1,0:T(8,128)S(1)}, f32[72,128]{1,0:T(8,128)S(1)}, u32[]{:S(2)}, u32[]{:S(2)}) collective-permute-start(f32[72,128]{1,0:T(8,128)S(1)} %shard_map.67.own), channel_id=1, source_target_pairs={{0,128},{16,144},{32,160},{48,176},{64,192},{80,208},{96,224},{112... | collective-permute-start | bytes 110600 | tf_op jit(solution)/shard_map/ppermute | solution.py:380
  36.8 5.3 %collective-permute-start.4 = (f32[72,128]{1,0:T(8,128)S(1)}, f32[72,128]{1,0:T(8,128)S(1)}, u32[]{:S(2)}, u32[]{:S(2)}) collective-permute-start(f32[72,128]{1,0:T(8,128)S(1)} %shard_map.67.own), channel_id=1, source_target_pairs={{128,0},{144,16},{160,32},{176,48},{192,64},{208,80},{224,96},{240... | collective-permute-start | bytes 110600 | tf_op jit(solution)/shard_map/ppermute | solution.py:381
  42.1 0.0 collective-permute-done.2.ahead1
  42.1 5.2 %collective-permute-start.3 = (f32[72,128]{1,0:T(8,128)S(1)}, f32[72,128]{1,0:T(8,128)S(1)}, u32[]{:S(2)}, u32[]{:S(2)}) collective-permute-start(f32[72,128]{1,0:T(8,128)S(1)} %collective-permute-done.2.ahead1), channel_id=1, source_target_pairs={{0,128},{16,144},{32,160},{48,176},{64,192},{80,208},{96,224},{112... | collective-permute-start | bytes 110600 | tf_op jit(solution)/shard_map/ppermute | solution.py:382
  47.3 0.3 collective-permute-done.4.ahead3
  47.6 3.1 %collective-permute-done.3.ahead2 = f32[72,128]{1,0:T(8,128)S(1)} collective-permute-done((f32[72,128]{1,0:T(8,128)S(1)}, f32[72,128]{1,0:T(8,128)S(1)}, u32[]{:S(2)}, u32[]{:S(2)}) %collective-permute-start.3) | collective-permute-done | bytes 36896 | tf_op jit(solution)/shard_map/ppermute | solution.py:382
  50.7 3.6 %shard_map.68 = f32[256,256]{1,0:T(8,128)S(1)} custom-call(s32[3]{0:T(128)S(1)} %pad_add_fusion.scalars, f32[72,128]{1,0:T(8,128)S(1)} %shard_map.67.own, f32[72,128]{1,0:T(8,128)S(1)} %collective-permute-done.2.ahead1, f32[72,128]{1,0:T(8,128)S(1)} %collective-permute-done.3.ahead2, f32[72,128]{1,0:T(8,128)S(1)} %collective-permute-done.4.ahead3, ...), custom_call_target="tpu_custom_call" | custom-call | flops 1000000 | bytes 500000 | tf_op jit(solution)/shard_map/pallas_call | solution.py:334
  54.3 11.6 %all_to_all.11.arrived = f32[8,32,256]{2,1,0:T(8,128)S(1)} all-to-all(f32[8,32,256]{2,1,0:T(8,128)S(1)} %bitcast.8), channel_id=1, replica_groups={{0,16,32,48,64,80,96,112},{128,144,160,176,192,208,224,240},{256,272,28..., dimensions={0} | all-to-all | bytes 524288 | tf_op jit(solution)/shard_map/all_to_all | solution.py:390
  65.9 0.9 %shard_map.69 = f32[32,8,256]{2,1,0:T(8,128)} custom-call(f32[8,32,256]{2,1,0:T(8,128)S(1)} %all_to_all.11.arrived), custom_call_target="tpu_custom_call" | custom-call | flops 1000000 | bytes 500000 | tf_op jit(solution)/shard_map/pallas_call | solution.py:334
  (1 shorter events, 0.0 us)
Async XLA Ops:
  0.0 7.5 %copy-start = (s32[1,32,256]{2,1,0:T(8,128)S(1)}, s32[1,32,256]{2,1,0:T(8,128)}, u32[]{:S(2)}) copy-start(s32[1,32,256]{2,1,0:T(8,128)} %cells.1) | copy-start | bytes 98308
  1.1 6.4 %collective-permute-start.1 = (f32[136,256]{1,0:T(8,128)S(1)}, f32[136,256]{1,0:T(8,128)S(1)}, u32[]{:S(2)}, u32[]{:S(2)}) collective-permute-start(f32[136,256]{1,0:T(8,128)S(1)} %get-tuple-element.10.bottom), channel_id=1, source_target_pairs={{0,1},{1,2},{2,3},{3,4},{4,5},{5,6},{6,7},{7,8},{8,9},{9,10},{10,1... | collective-permute-start | bytes 417800 | tf_op jit(solution)/shard_map/ppermute | solution.py:360
  5.4 8.1 %collective-permute-start = (f32[136,256]{1,0:T(8,128)S(1)}, f32[136,256]{1,0:T(8,128)S(1)}, u32[]{:S(2)}, u32[]{:S(2)}) collective-permute-start(f32[136,256]{1,0:T(8,128)S(1)} %get-tuple-element.11.top), channel_id=1, source_target_pairs={{1,0},{2,1},{3,2},{4,3},{5,4},{6,5},{7,6},{8,7},{9,8},{10,9},{11,1... | collective-permute-start | bytes 417800 | tf_op jit(solution)/shard_map/ppermute | solution.py:361
  7.4 0.7 %copy-start.1 = (f32[1,1,256]{2,1,0:T(1,128)S(1)}, f32[1,1,256]{2,1,0:T(1,128)}, u32[]{:S(2)}) copy-start(f32[1,1,256]{2,1,0:T(1,128)} %values.1) | copy-start | bytes 3076
  7.4 0.7 %copy-start.2 = (f32[1,1,256]{2,1,0:T(1,128)S(1)}, f32[1,1,256]{2,1,0:T(1,128)}, u32[]{:S(2)}) copy-start(f32[1,1,256]{2,1,0:T(1,128)} %variances.1) | copy-start | bytes 3076
  28.0 14.2 %collective-permute-start.2 = (f32[72,128]{1,0:T(8,128)S(1)}, f32[72,128]{1,0:T(8,128)S(1)}, u32[]{:S(2)}, u32[]{:S(2)}) collective-permute-start(f32[72,128]{1,0:T(8,128)S(1)} %shard_map.67.own), channel_id=1, source_target_pairs={{0,128},{16,144},{32,160},{48,176},{64,192},{80,208},{96,224},{112... | collective-permute-start | bytes 110600 | tf_op jit(solution)/shard_map/ppermute | solution.py:380
  36.8 10.8 %collective-permute-start.4 = (f32[72,128]{1,0:T(8,128)S(1)}, f32[72,128]{1,0:T(8,128)S(1)}, u32[]{:S(2)}, u32[]{:S(2)}) collective-permute-start(f32[72,128]{1,0:T(8,128)S(1)} %shard_map.67.own), channel_id=1, source_target_pairs={{128,0},{144,16},{160,32},{176,48},{192,64},{208,80},{224,96},{240... | collective-permute-start | bytes 110600 | tf_op jit(solution)/shard_map/ppermute | solution.py:381
  42.1 8.6 %collective-permute-start.3 = (f32[72,128]{1,0:T(8,128)S(1)}, f32[72,128]{1,0:T(8,128)S(1)}, u32[]{:S(2)}, u32[]{:S(2)}) collective-permute-start(f32[72,128]{1,0:T(8,128)S(1)} %collective-permute-done.2.ahead1), channel_id=1, source_target_pairs={{0,128},{16,144},{32,160},{48,176},{64,192},{80,208},{96,224},{112... | collective-permute-start | bytes 110600 | tf_op jit(solution)/shard_map/ppermute | solution.py:382

commit v4 on v3

--- a/solution.py
+++ b/solution.py
@@ -42,12 +42,12 @@
         out[pl.ds(STEPS * members, 2 * STEPS), :] = jnp.concatenate([edge, edge], axis=0)
 
 
-def observe(scalars, cells, values, variances, out):
+def observe(count, cells, values, variances, out):
     slots = values.shape[2]
-    live = lax.broadcasted_iota(jnp.int32, (1, slots), 1) < scalars[1]
+    live = lax.broadcasted_iota(jnp.int32, (1, slots), 1) < count[...]
     weight = jnp.where(live, 1.0 / variances[0], 0.0)
     scaled = weight * values[0]
-    mine = cells[0, pl.ds(scalars[0], 1), :]
+    mine = cells[0, pl.ds(lax.axis_index("mem"), 1), :]
     cell = lax.broadcasted_iota(jnp.int32, (2 * CELLS, slots), 0) % CELLS
     hit = jnp.where(cell == mine, 1.0, 0.0)
     row = lax.broadcasted_iota(jnp.int32, (8, slots), 0)
@@ -90,10 +90,10 @@
         out[near, pl.ds(tile * first.shape[0], first.shape[0]), pl.ds(lanes_at, LANES)] = joined
 
 
-def early_kernel(last_strip, scalars, cells, values, variances, before, top, bottom, out, kept, observed):
-    observe(scalars, cells, values, variances, observed)
+def early_kernel(last_strip, count, cells, values, variances, before, top, bottom, out, kept, observed):
+    observe(count, cells, values, variances, observed)
     members = out.shape[1]
-    strip = scalars[2]
+    strip = lax.axis_index("lat")
     sources = [before, top, bottom]
 
     def forces(place):
@@ -112,9 +112,9 @@
         spread_patches(out, 0, tile, [rows[place] for place in range(4, 8)])
 
 
-def late_kernel(last_strip, scalars, bottom, after, kept, early, out):
+def late_kernel(last_strip, bottom, after, kept, early, out):
     members = out.shape[1]
-    strip = scalars[2]
+    strip = lax.axis_index("lat")
     sources = [None, None, bottom, after]
 
     def forces(place):
@@ -252,26 +252,21 @@
                     pair[place] = rest
 
 
-def analyse_kernel(scalars, own, ahead1, ahead2, ahead3, states, out):
+def analyse_kernel(received, states, out):
     group = states.shape[0]
     members = FAR * group
     side = CELLS // 2
-    received = (own, ahead1, ahead2, ahead3)
-
-    def line(back, place):
-        return received[back][pl.ds(CELLS + place, 1), :]
+
+    def line(hi, place):
+        return received[hi // 2, pl.ds(CELLS + 8 * (hi % 2) + place, 1), :]
 
     def observed(hi):
-        back = (scalars[0] // NEAR + FAR - hi) % FAR
-        value = line(0, 4)
-        for place in range(1, FAR):
-            value = jnp.where(back == place, line(place, 4), value)
-        return value
+        return line(hi, 4)
 
     def total(part):
         return part(0) + part(1) + part(2) + part(3)
 
-    packed = [total(lambda back: received[back][pl.ds(half * side, side), :]) for half in range(2)]
+    packed = [received[0, pl.ds(half * side, side), :] + received[1, pl.ds(half * side, side), :] for half in range(2)]
     within = unpack_symmetric(packed, [total(lambda hi: line(hi, 2 * half + 1)) for half in range(2)])
     row, lane = places((CELLS, LANES))
     identity = jnp.where(row == lane, 1.0, 0.0)
@@ -324,7 +319,6 @@
 
 
 VMEM = pl.BlockSpec(memory_space=pltpu.VMEM)
-SMEM = pl.BlockSpec(memory_space=pltpu.SMEM)
 HBM = pl.BlockSpec(memory_space=pltpu.HBM)
 
 
@@ -345,7 +339,6 @@
 def local(fields, forcing, obs_cell, obs_count, obs_value, obs_var):
     members, rows, lon = fields.shape
     strips = lax.axis_size("lat")
-    scalars = jnp.stack([lax.axis_index("mem"), obs_count[0, 0], lax.axis_index("lat")]).astype(jnp.int32)
     height = STEPS * members + 2 * STEPS
     fields, forcing = (pltpu.with_memory_space_constraint(value, pltpu.HBM) for value in (fields, forcing))
     top, bottom = call(
@@ -362,30 +355,28 @@
     early, kept, observed = call(
         functools.partial(early_kernel, strips - 1),
         [(NEAR, members, LANES), (6, members, lon), (8, LANES)],
-        [SMEM] + [VMEM] * 6,
-        (scalars, obs_cell, obs_value, obs_var, before, top, bottom),
+        [VMEM] * 7,
+        (obs_count, obs_cell, obs_value, obs_var, before, top, bottom),
         flops=10_000_000,
     )
     states = call(
         functools.partial(late_kernel, strips - 1),
         (NEAR, members, lon),
-        [SMEM, VMEM, VMEM, VMEM, VMEM],
-        (scalars, bottom, after, kept, early),
+        [VMEM] * 4,
+        (bottom, after, kept, early),
     )
     states = lax.all_to_all(states, "mem", 0, 0, axis_index_groups=NEAR_GROUPS, tiled=True)
     states = states.reshape(NEAR * members, lon)
     partial = call(moments_kernel, (CELLS + 8, LANES), [VMEM, VMEM], (states, observed))
-    size = FAR * NEAR
-    onward = [(i, (i + NEAR) % size) for i in range(size)]
-    ahead1 = lax.ppermute(partial, "mem", onward)
-    ahead3 = lax.ppermute(partial, "mem", [(j, i) for i, j in onward])
-    ahead2 = lax.ppermute(ahead1, "mem", onward)
-    result = call(
-        analyse_kernel,
-        states.shape,
-        [SMEM] + [VMEM] * (FAR + 1),
-        (scalars, partial, ahead1, ahead2, ahead3, states),
-    )
+    def exchange(value, *pairs):
+        groups = [[first * NEAR + near, second * NEAR + near] for first, second in pairs for near in range(NEAR)]
+        return lax.all_gather(value, "mem", axis_index_groups=groups)
+
+    near_pair = exchange(partial, (0, 1), (2, 3))
+    summed = near_pair[0, :CELLS] + near_pair[1, :CELLS]
+    merged = jnp.concatenate([summed, near_pair[0, CELLS:], near_pair[1, CELLS:]], axis=0)
+    received = exchange(merged, (0, 3), (1, 2))
+    result = call(analyse_kernel, states.shape, [VMEM, VMEM], (received, states))
     result = result.reshape(NEAR, members, lon)
     result = lax.all_to_all(result, "mem", 0, 0, axis_index_groups=NEAR_GROUPS, tiled=True)
     return call(unpack_kernel, (members, rows, lon), [VMEM], (result,))

time: 67.6 us -> 64.3 us (0.951)
  blocking collectives: 24.3 us -> 45.3 us
  starting transfers between devices: 25 us -> 5.66 us
  waiting for transfers between devices: 7.43 us -> 5.23 us
  Pallas kernels: 8.69 us -> 7.02 us
    all_gather x0 -> x2, blocking collectives: none -> 20.4 us  [exchange(): return lax.all_gather(value, 'mem', axis_index_groups=groups)]
    ppermute x3 -> x0, starting transfers between devices: 19.3 us -> none  [the longest x1 8.81 us: local(): ahead1 = lax.ppermute(partial, 'mem', onward)]
    ppermute x3 -> x0, waiting for transfers between devices: 3.43 us -> none  [the longest x1 3.14 us: local(): ahead2 = lax.ppermute(ahead1, 'mem', onward)]
    pallas_call x6, Pallas kernels: 8.69 us -> 7.02 us  [call(): pl.pallas_call(kernel, out_shape=shapes if many else shapes[0], in_specs=...]
    ppermute x1, waiting for transfers between devices: 4.01 us -> 5.2 us  [local(): after = lax.ppermute(top, 'lat', down)]
  transfers between devices with their start and end apart: 5 -> 2, of which waited for: 3 -> 1; matrix products, arithmetic and copies ran while one was open for 0% -> 0% of each run, Pallas kernels for 2% -> 1%
where the time goes in v4:
time: 64.3 us; the launch traced here: 64 us
  blocking collectives  45.3 us (70%)
  Pallas kernels  7.02 us (11%)
  starting transfers between devices  5.66 us (9%)
  waiting for transfers between devices  5.23 us (8%)
  between operations  0.73 us (1%)
    all_gather x2, blocking collectives, exchange(): return lax.all_gather(value, 'mem', axis_index_groups=groups)  20.4 us
    all_to_all x1, blocking collectives, local(): lax.all_to_all(states, 'mem', 0, 0, axis_index_groups=NEAR_GROUPS, tiled=...  12.7 us
    all_to_all x1, blocking collectives, local(): lax.all_to_all(result, 'mem', 0, 0, axis_index_groups=NEAR_GROUPS, tiled=...  12.2 us
    pallas_call x6, Pallas kernels, call(): pl.pallas_call(kernel, out_shape=shapes if many else shapes[0], in_specs=...  7.02 us
    ppermute x1, waiting for transfers between devices, local(): after = lax.ppermute(top, 'lat', down)  5.2 us
    ppermute x1, starting transfers between devices, local(): before = lax.ppermute(bottom, 'lat', up)  4.37 us
    ppermute x1, starting transfers between devices, local(): after = lax.ppermute(top, 'lat', down)  1.29 us
  transfers between devices with their start and end apart: 2, of which 1 were waited for; matrix products, arithmetic and copies ran while one was open for 0% of the time, Pallas kernels for 1%

profile of v4, /device:TPU:1, one launch (start us, length us, event | category | flops | bytes accessed | tf_op | source)
XLA Modules:
  0.0 64.0 jit_solution(14771380102585515944)
XLA Ops:
  0.0 0.0 copy-start
  0.0 1.1 %shard_map.64 = (f32[136,256]{1,0:T(8,128)S(1)}, f32[136,256]{1,0:T(8,128)S(1)}) custom-call(f32[32,8,256]{2,1,0:T(8,128)} %fields.1, f32[8,256]{1,0:T(8,128)} %forcing.1), custom_call_target="tpu_custom_call" | custom-call | flops 1000000 | bytes 500000 | tf_op jit(solution)/shard_map/pallas_call | solution.py:328
  1.1 4.4 %collective-permute-start.1 = (f32[136,256]{1,0:T(8,128)S(1)}, f32[136,256]{1,0:T(8,128)S(1)}, u32[]{:S(2)}, u32[]{:S(2)}) collective-permute-start(f32[136,256]{1,0:T(8,128)S(1)} %get-tuple-element.10.bottom), channel_id=1, source_target_pairs={{0,1},{1,2},{2,3},{3,4},{4,5},{5,6},{6,7},{7,8},{8,9},{9,10},{10,1... | collective-permute-start | bytes 417800 | tf_op jit(solution)/shard_map/ppermute | solution.py:353
  5.4 0.0 copy-start.2
  5.5 0.0 copy-start.1
  5.5 1.3 %collective-permute-start = (f32[136,256]{1,0:T(8,128)S(1)}, f32[136,256]{1,0:T(8,128)S(1)}, u32[]{:S(2)}, u32[]{:S(2)}) collective-permute-start(f32[136,256]{1,0:T(8,128)S(1)} %get-tuple-element.11.top), channel_id=1, source_target_pairs={{1,0},{2,1},{3,2},{4,3},{5,4},{6,5},{7,6},{8,7},{9,8},{10,9},{11,1... | collective-permute-start | bytes 417800 | tf_op jit(solution)/shard_map/ppermute | solution.py:354
  7.4 0.0 collective-permute-done.1.before
  7.4 0.0 copy-done
  7.4 0.0 copy-done.2
  7.5 0.0 copy-done.1
  7.5 0.9 %shard_map.65 = (f32[8,32,128]{2,1,0:T(8,128)S(1)}, f32[6,32,256]{2,1,0:T(8,128)S(1)}, f32[8,128]{1,0:T(8,128)S(1)}) custom-call(s32[1,1]{1,0:T(1,128)S(6)} %copy.7.count, s32[1,32,256]{2,1,0:T(8,128)S(1)} %copy-done, f32[1,1,256]{2,1,0:T(1,128)S(1)} %copy-done.1, f32[1,1,256]{2,1,0:T(1,128)S(1)} %copy-done.2, f32[136,256]{1,0:T(8,128)S(1)} %collective-permute-done.1.before, ...), custom_call_target="tpu_custom_call" | custom-call | flops 10000000 | bytes 500000 | tf_op jit(solution)/shard_map/pallas_call | solution.py:328
  8.4 5.2 %collective-permute-done.after = f32[136,256]{1,0:T(8,128)S(1)} collective-permute-done((f32[136,256]{1,0:T(8,128)S(1)}, f32[136,256]{1,0:T(8,128)S(1)}, u32[]{:S(2)}, u32[]{:S(2)}) %collective-permute-start) | collective-permute-done | bytes 139296 | tf_op jit(solution)/shard_map/ppermute | solution.py:354
  13.6 0.6 shard_map.66
  14.1 12.7 %all_to_all.10 = f32[8,32,256]{2,1,0:T(8,128)S(1)} all-to-all(f32[8,32,256]{2,1,0:T(8,128)S(1)} %shard_map.66), channel_id=1, replica_groups={{0,16,32,48,64,80,96,112},{128,144,160,176,192,208,224,240},{256,272,28..., dimensions={0} | all-to-all | bytes 524288 | tf_op jit(solution)/shard_map/all_to_all | solution.py:368
  26.9 0.5 shard_map.67
  27.4 9.7 %all-gather = f32[144,128]{1,0:T(8,128)S(1)} all-gather(f32[72,128]{1,0:T(8,128)S(1)} %shard_map.67), channel_id=2, replica_groups={{0,128},{16,144},{32,160},{48,176},{64,192},{80,208},{96,224},{112,240}..., dimensions={0}, use_global_device_ids=true | all-gather | bytes 110592 | tf_op jit(solution)/shard_map/all_gather | solution.py:373
  37.1 10.7 %all-gather.1 = f32[160,128]{1,0:T(8,128)S(1)} all-gather(f32[80,128]{1,0:T(8,128)S(1)} %pad_maximum_fusion), channel_id=3, replica_groups={{0,384},{16,400},{32,416},{48,432},{64,448},{80,464},{96,480},{112,496}..., dimensions={0}, use_global_device_ids=true | all-gather | bytes 122880 | tf_op jit(solution)/shard_map/all_gather | solution.py:373
  47.8 3.0 %shard_map.68 = f32[256,256]{1,0:T(8,128)S(1)} custom-call(f32[2,80,128]{2,1,0:T(8,128)S(1)} %bitcast.13, f32[256,256]{1,0:T(8,128)S(1)} %bitcast.11), custom_call_target="tpu_custom_call" | custom-call | flops 1000000 | bytes 500000 | tf_op jit(solution)/shard_map/pallas_call | solution.py:328
  50.8 12.2 %all_to_all.11.arrived = f32[8,32,256]{2,1,0:T(8,128)S(1)} all-to-all(f32[8,32,256]{2,1,0:T(8,128)S(1)} %bitcast.12), channel_id=1, replica_groups={{0,16,32,48,64,80,96,112},{128,144,160,176,192,208,224,240},{256,272,28..., dimensions={0} | all-to-all | bytes 524288 | tf_op jit(solution)/shard_map/all_to_all | solution.py:381
  63.1 0.9 %shard_map.69 = f32[32,8,256]{2,1,0:T(8,128)} custom-call(f32[8,32,256]{2,1,0:T(8,128)S(1)} %all_to_all.11.arrived), custom_call_target="tpu_custom_call" | custom-call | flops 1000000 | bytes 500000 | tf_op jit(solution)/shard_map/pallas_call | solution.py:328
  (3 shorter events, 0.0 us)
Async XLA Ops:
  0.0 7.4 %copy-start = (s32[1,32,256]{2,1,0:T(8,128)S(1)}, s32[1,32,256]{2,1,0:T(8,128)}, u32[]{:S(2)}) copy-start(s32[1,32,256]{2,1,0:T(8,128)} %cells.1) | copy-start | bytes 98308
  1.1 6.4 %collective-permute-start.1 = (f32[136,256]{1,0:T(8,128)S(1)}, f32[136,256]{1,0:T(8,128)S(1)}, u32[]{:S(2)}, u32[]{:S(2)}) collective-permute-start(f32[136,256]{1,0:T(8,128)S(1)} %get-tuple-element.10.bottom), channel_id=1, source_target_pairs={{0,1},{1,2},{2,3},{3,4},{4,5},{5,6},{6,7},{7,8},{8,9},{9,10},{10,1... | collective-permute-start | bytes 417800 | tf_op jit(solution)/shard_map/ppermute | solution.py:353
  5.4 2.0 %copy-start.2 = (f32[1,1,256]{2,1,0:T(1,128)S(1)}, f32[1,1,256]{2,1,0:T(1,128)}, u32[]{:S(2)}) copy-start(f32[1,1,256]{2,1,0:T(1,128)} %variances.1) | copy-start | bytes 3076
  5.5 2.0 %copy-start.1 = (f32[1,1,256]{2,1,0:T(1,128)S(1)}, f32[1,1,256]{2,1,0:T(1,128)}, u32[]{:S(2)}) copy-start(f32[1,1,256]{2,1,0:T(1,128)} %values.1) | copy-start | bytes 3076
  5.5 8.1 %collective-permute-start = (f32[136,256]{1,0:T(8,128)S(1)}, f32[136,256]{1,0:T(8,128)S(1)}, u32[]{:S(2)}, u32[]{:S(2)}) collective-permute-start(f32[136,256]{1,0:T(8,128)S(1)} %get-tuple-element.11.top), channel_id=1, source_target_pairs={{1,0},{2,1},{3,2},{4,3},{5,4},{6,5},{7,6},{8,7},{9,8},{10,9},{11,1... | collective-permute-start | bytes 417800 | tf_op jit(solution)/shard_map/ppermute | solution.py:354

commit v5 on v4

--- a/solution.py
+++ b/solution.py
@@ -174,17 +174,17 @@
 
 
 def moments_kernel(states, observed, out):
+    mean = jnp.sum(states[...], axis=0, keepdims=True) / states.shape[0]
+    centred = states[...] - mean
+    square = lax.dot_general(
+        centred, centred, (((0,), (0,)), ((), ())), precision=HIGHEST, preferred_element_type=jnp.float32
+    )
     lines = []
     for half in range(2):
-        block = states[:, pl.ds(half * LANES, LANES)]
-        mean = jnp.sum(block, axis=0, keepdims=True) / block.shape[0]
-        centred = block - mean
-        square = lax.dot_general(
-            centred, centred, (((0,), (0,)), ((), ())), precision=HIGHEST, preferred_element_type=jnp.float32
-        )
-        packed, diagonal = pack_symmetric(fold(square))
+        lanes = slice(half * LANES, half * LANES + LANES)
+        packed, diagonal = pack_symmetric(fold(square[lanes, lanes]))
         out[pl.ds(half * CELLS // 2, CELLS // 2), :] = packed
-        lines += [mean, diagonal]
+        lines += [mean[:, lanes], diagonal]
     row = lax.broadcasted_iota(jnp.int32, (8, LANES), 0)
     tail = observed[...]
     for place, line in enumerate(lines):
@@ -295,17 +295,20 @@
         shifts.append(shift[:1])
         pairs.append([system[8 * tile:8 * tile + 8] for tile in range(8)])
     invert(pairs)
-    for half in range(2):
-        block = states[:, pl.ds(half * LANES, LANES)]
-        spread = 0.5 * (block - means[half])
-        gain = unfold(jnp.concatenate(pairs[half], axis=0))
-        out[:, pl.ds(half * LANES, LANES)] = (block - spread) + lax.dot_general(
-            spread + shifts[half],
-            gain,
-            (((1,), (1,)), ((), ())),
-            precision=HIGHEST,
-            preferred_element_type=jnp.float32,
-        )
+    block = states[...]
+    spread = 0.5 * (block - jnp.concatenate(means, axis=1))
+    gains = [unfold(jnp.concatenate(pair, axis=0)) for pair in pairs]
+    empty = jnp.zeros((LANES, LANES), jnp.float32)
+    gain = jnp.concatenate(
+        [jnp.concatenate([gains[0], empty], axis=1), jnp.concatenate([empty, gains[1]], axis=1)], axis=0
+    )
+    out[...] = (block - spread) + lax.dot_general(
+        spread + jnp.concatenate(shifts, axis=1),
+        gain,
+        (((1,), (1,)), ((), ())),
+        precision=HIGHEST,
+        preferred_element_type=jnp.float32,
+    )
 
 
 def unpack_kernel(arrived, out):

time: 64.3 us -> 64 us (level)
  no operation moved by 1% of the time
where the time goes in v5:
time: 64 us; the launch traced here: 63.7 us
  blocking collectives  45.3 us (71%)
  Pallas kernels  6.76 us (11%)
  starting transfers between devices  5.66 us (9%)
  waiting for transfers between devices  5.23 us (8%)
  between operations  0.73 us (1%)
    all_gather x2, blocking collectives, exchange(): return lax.all_gather(value, 'mem', axis_index_groups=groups)  20.4 us
    all_to_all x1, blocking collectives, local(): lax.all_to_all(states, 'mem', 0, 0, axis_index_groups=NEAR_GROUPS, tiled=...  12.7 us
    all_to_all x1, blocking collectives, local(): lax.all_to_all(result, 'mem', 0, 0, axis_index_groups=NEAR_GROUPS, tiled=...  12.2 us
    pallas_call x6, Pallas kernels, call(): pl.pallas_call(kernel, out_shape=shapes if many else shapes[0], in_specs=...  6.76 us
    ppermute x1, waiting for transfers between devices, local(): after = lax.ppermute(top, 'lat', down)  5.2 us
    ppermute x1, starting transfers between devices, local(): before = lax.ppermute(bottom, 'lat', up)  4.37 us
    ppermute x1, starting transfers between devices, local(): after = lax.ppermute(top, 'lat', down)  1.29 us
  transfers between devices with their start and end apart: 2, of which 1 were waited for; matrix products, arithmetic and copies ran while one was open for 0% of the time, Pallas kernels for 1%

profile of v5, /device:TPU:1, one launch (start us, length us, event | category | flops | bytes accessed | tf_op | source)
XLA Modules:
  0.0 63.7 jit_solution(1459001130855798108)
XLA Ops:
  0.0 0.0 copy-start
  0.0 1.1 %shard_map.64 = (f32[136,256]{1,0:T(8,128)S(1)}, f32[136,256]{1,0:T(8,128)S(1)}) custom-call(f32[32,8,256]{2,1,0:T(8,128)} %fields.1, f32[8,256]{1,0:T(8,128)} %forcing.1), custom_call_target="tpu_custom_call" | custom-call | flops 1000000 | bytes 500000 | tf_op jit(solution)/shard_map/pallas_call | solution.py:331
  1.1 4.4 %collective-permute-start.1 = (f32[136,256]{1,0:T(8,128)S(1)}, f32[136,256]{1,0:T(8,128)S(1)}, u32[]{:S(2)}, u32[]{:S(2)}) collective-permute-start(f32[136,256]{1,0:T(8,128)S(1)} %get-tuple-element.10.bottom), channel_id=1, source_target_pairs={{0,1},{1,2},{2,3},{3,4},{4,5},{5,6},{6,7},{7,8},{8,9},{9,10},{10,1... | collective-permute-start | bytes 417800 | tf_op jit(solution)/shard_map/ppermute | solution.py:356
  5.4 0.0 copy-start.2
  5.5 0.0 copy-start.1
  5.5 1.3 %collective-permute-start = (f32[136,256]{1,0:T(8,128)S(1)}, f32[136,256]{1,0:T(8,128)S(1)}, u32[]{:S(2)}, u32[]{:S(2)}) collective-permute-start(f32[136,256]{1,0:T(8,128)S(1)} %get-tuple-element.11.top), channel_id=1, source_target_pairs={{1,0},{2,1},{3,2},{4,3},{5,4},{6,5},{7,6},{8,7},{9,8},{10,9},{11,1... | collective-permute-start | bytes 417800 | tf_op jit(solution)/shard_map/ppermute | solution.py:357
  7.4 0.0 collective-permute-done.1.before
  7.4 0.0 copy-done
  7.4 0.0 copy-done.2
  7.5 0.0 copy-done.1
  7.5 0.9 %shard_map.65 = (f32[8,32,128]{2,1,0:T(8,128)S(1)}, f32[6,32,256]{2,1,0:T(8,128)S(1)}, f32[8,128]{1,0:T(8,128)S(1)}) custom-call(s32[1,1]{1,0:T(1,128)S(6)} %copy.7.count, s32[1,32,256]{2,1,0:T(8,128)S(1)} %copy-done, f32[1,1,256]{2,1,0:T(1,128)S(1)} %copy-done.1, f32[1,1,256]{2,1,0:T(1,128)S(1)} %copy-done.2, f32[136,256]{1,0:T(8,128)S(1)} %collective-permute-done.1.before, ...), custom_call_target="tpu_custom_call" | custom-call | flops 10000000 | bytes 500000 | tf_op jit(solution)/shard_map/pallas_call | solution.py:331
  8.4 5.2 %collective-permute-done.after = f32[136,256]{1,0:T(8,128)S(1)} collective-permute-done((f32[136,256]{1,0:T(8,128)S(1)}, f32[136,256]{1,0:T(8,128)S(1)}, u32[]{:S(2)}, u32[]{:S(2)}) %collective-permute-start) | collective-permute-done | bytes 139296 | tf_op jit(solution)/shard_map/ppermute | solution.py:357
  13.6 0.6 shard_map.66
  14.1 12.7 %all_to_all.10 = f32[8,32,256]{2,1,0:T(8,128)S(1)} all-to-all(f32[8,32,256]{2,1,0:T(8,128)S(1)} %shard_map.66), channel_id=1, replica_groups={{0,16,32,48,64,80,96,112},{128,144,160,176,192,208,224,240},{256,272,28..., dimensions={0} | all-to-all | bytes 524288 | tf_op jit(solution)/shard_map/all_to_all | solution.py:371
  26.9 0.5 shard_map.67
  27.4 9.7 %all-gather = f32[144,128]{1,0:T(8,128)S(1)} all-gather(f32[72,128]{1,0:T(8,128)S(1)} %shard_map.67), channel_id=2, replica_groups={{0,128},{16,144},{32,160},{48,176},{64,192},{80,208},{96,224},{112,240}..., dimensions={0}, use_global_device_ids=true | all-gather | bytes 110592 | tf_op jit(solution)/shard_map/all_gather | solution.py:376
  37.1 10.7 %all-gather.1 = f32[160,128]{1,0:T(8,128)S(1)} all-gather(f32[80,128]{1,0:T(8,128)S(1)} %pad_maximum_fusion), channel_id=3, replica_groups={{0,384},{16,400},{32,416},{48,432},{64,448},{80,464},{96,480},{112,496}..., dimensions={0}, use_global_device_ids=true | all-gather | bytes 122880 | tf_op jit(solution)/shard_map/all_gather | solution.py:376
  47.8 2.8 %shard_map.68 = f32[256,256]{1,0:T(8,128)S(1)} custom-call(f32[2,80,128]{2,1,0:T(8,128)S(1)} %bitcast.13, f32[256,256]{1,0:T(8,128)S(1)} %bitcast.11), custom_call_target="tpu_custom_call" | custom-call | flops 1000000 | bytes 500000 | tf_op jit(solution)/shard_map/pallas_call | solution.py:331
  50.6 12.2 %all_to_all.11.arrived = f32[8,32,256]{2,1,0:T(8,128)S(1)} all-to-all(f32[8,32,256]{2,1,0:T(8,128)S(1)} %bitcast.12), channel_id=1, replica_groups={{0,16,32,48,64,80,96,112},{128,144,160,176,192,208,224,240},{256,272,28..., dimensions={0} | all-to-all | bytes 524288 | tf_op jit(solution)/shard_map/all_to_all | solution.py:384
  62.8 0.9 %shard_map.69 = f32[32,8,256]{2,1,0:T(8,128)} custom-call(f32[8,32,256]{2,1,0:T(8,128)S(1)} %all_to_all.11.arrived), custom_call_target="tpu_custom_call" | custom-call | flops 1000000 | bytes 500000 | tf_op jit(solution)/shard_map/pallas_call | solution.py:331
  (3 shorter events, 0.0 us)
Async XLA Ops:
  0.0 7.4 %copy-start = (s32[1,32,256]{2,1,0:T(8,128)S(1)}, s32[1,32,256]{2,1,0:T(8,128)}, u32[]{:S(2)}) copy-start(s32[1,32,256]{2,1,0:T(8,128)} %cells.1) | copy-start | bytes 98308
  1.1 6.4 %collective-permute-start.1 = (f32[136,256]{1,0:T(8,128)S(1)}, f32[136,256]{1,0:T(8,128)S(1)}, u32[]{:S(2)}, u32[]{:S(2)}) collective-permute-start(f32[136,256]{1,0:T(8,128)S(1)} %get-tuple-element.10.bottom), channel_id=1, source_target_pairs={{0,1},{1,2},{2,3},{3,4},{4,5},{5,6},{6,7},{7,8},{8,9},{9,10},{10,1... | collective-permute-start | bytes 417800 | tf_op jit(solution)/shard_map/ppermute | solution.py:356
  5.4 2.0 %copy-start.2 = (f32[1,1,256]{2,1,0:T(1,128)S(1)}, f32[1,1,256]{2,1,0:T(1,128)}, u32[]{:S(2)}) copy-start(f32[1,1,256]{2,1,0:T(1,128)} %variances.1) | copy-start | bytes 3076
  5.5 2.0 %copy-start.1 = (f32[1,1,256]{2,1,0:T(1,128)S(1)}, f32[1,1,256]{2,1,0:T(1,128)}, u32[]{:S(2)}) copy-start(f32[1,1,256]{2,1,0:T(1,128)} %values.1) | copy-start | bytes 3076
  5.5 8.1 %collective-permute-start = (f32[136,256]{1,0:T(8,128)S(1)}, f32[136,256]{1,0:T(8,128)S(1)}, u32[]{:S(2)}, u32[]{:S(2)}) collective-permute-start(f32[136,256]{1,0:T(8,128)S(1)} %get-tuple-element.11.top), channel_id=1, source_target_pairs={{1,0},{2,1},{3,2},{4,3},{5,4},{6,5},{7,6},{8,7},{9,8},{10,9},{11,1... | collective-permute-start | bytes 417800 | tf_op jit(solution)/shard_map/ppermute | solution.py:357

commit v6 on v5

--- a/solution.py
+++ b/solution.py
@@ -283,16 +283,11 @@
         covariance = (within[half] + group * fold(between)) / (members - 1)
         first, second = observed(2 * half), observed(2 * half + 1)
         weight = halves(first, 0, second, 0)
-        shift = halves(first, 1, second, 1) - weight * mean
-        shift = jnp.dot(
-            jnp.broadcast_to(shift, (8, LANES)),
-            unfold(covariance),
-            precision=HIGHEST,
-            preferred_element_type=jnp.float32,
-        )
+        seen = weight > 0.0
+        target = halves(first, 1, second, 1) / jnp.where(seen, weight, 1.0)
+        shifts.append(jnp.where(seen, target - mean, 0.0))
         system = covariance * weight + identity
         means.append(mean)
-        shifts.append(shift[:1])
         pairs.append([system[8 * tile:8 * tile + 8] for tile in range(8)])
     invert(pairs)
     block = states[...]
@@ -302,8 +297,9 @@
     gain = jnp.concatenate(
         [jnp.concatenate([gains[0], empty], axis=1), jnp.concatenate([empty, gains[1]], axis=1)], axis=0
     )
-    out[...] = (block - spread) + lax.dot_general(
-        spread + jnp.concatenate(shifts, axis=1),
+    shift = jnp.concatenate(shifts, axis=1)
+    out[...] = (block - spread) + shift + lax.dot_general(
+        spread - shift,
         gain,
         (((1,), (1,)), ((), ())),
         precision=HIGHEST,

time: 64 us -> 64 us (level)
  no operation moved by 1% of the time
where the time goes in v6:
time: 64 us; the launch traced here: 63.7 us
  blocking collectives  45.3 us (71%)
  Pallas kernels  6.74 us (11%)
  starting transfers between devices  5.66 us (9%)
  waiting for transfers between devices  5.23 us (8%)
  between operations  0.73 us (1%)
    all_gather x2, blocking collectives, exchange(): return lax.all_gather(value, 'mem', axis_index_groups=groups)  20.4 us
    all_to_all x1, blocking collectives, local(): lax.all_to_all(states, 'mem', 0, 0, axis_index_groups=NEAR_GROUPS, tiled=...  12.7 us
    all_to_all x1, blocking collectives, local(): lax.all_to_all(result, 'mem', 0, 0, axis_index_groups=NEAR_GROUPS, tiled=...  12.2 us
    pallas_call x6, Pallas kernels, call(): pl.pallas_call(kernel, out_shape=shapes if many else shapes[0], in_specs=...  6.74 us
    ppermute x1, waiting for transfers between devices, local(): after = lax.ppermute(top, 'lat', down)  5.2 us
    ppermute x1, starting transfers between devices, local(): before = lax.ppermute(bottom, 'lat', up)  4.37 us
    ppermute x1, starting transfers between devices, local(): after = lax.ppermute(top, 'lat', down)  1.29 us
  transfers between devices with their start and end apart: 2, of which 1 were waited for; matrix products, arithmetic and copies ran while one was open for 0% of the time, Pallas kernels for 1%

profile of v6, /device:TPU:1, one launch (start us, length us, event | category | flops | bytes accessed | tf_op | source)
XLA Modules:
  0.0 63.7 jit_solution(2329034529697506975)
XLA Ops:
  0.0 0.0 copy-start
  0.0 1.1 %shard_map.64 = (f32[136,256]{1,0:T(8,128)S(1)}, f32[136,256]{1,0:T(8,128)S(1)}) custom-call(f32[32,8,256]{2,1,0:T(8,128)} %fields.1, f32[8,256]{1,0:T(8,128)} %forcing.1), custom_call_target="tpu_custom_call" | custom-call | flops 1000000 | bytes 500000 | tf_op jit(solution)/shard_map/pallas_call | solution.py:327
  1.1 4.4 %collective-permute-start.1 = (f32[136,256]{1,0:T(8,128)S(1)}, f32[136,256]{1,0:T(8,128)S(1)}, u32[]{:S(2)}, u32[]{:S(2)}) collective-permute-start(f32[136,256]{1,0:T(8,128)S(1)} %get-tuple-element.10.bottom), channel_id=1, source_target_pairs={{0,1},{1,2},{2,3},{3,4},{4,5},{5,6},{6,7},{7,8},{8,9},{9,10},{10,1... | collective-permute-start | bytes 417800 | tf_op jit(solution)/shard_map/ppermute | solution.py:352
  5.4 0.0 copy-start.2
  5.5 0.0 copy-start.1
  5.5 1.3 %collective-permute-start = (f32[136,256]{1,0:T(8,128)S(1)}, f32[136,256]{1,0:T(8,128)S(1)}, u32[]{:S(2)}, u32[]{:S(2)}) collective-permute-start(f32[136,256]{1,0:T(8,128)S(1)} %get-tuple-element.11.top), channel_id=1, source_target_pairs={{1,0},{2,1},{3,2},{4,3},{5,4},{6,5},{7,6},{8,7},{9,8},{10,9},{11,1... | collective-permute-start | bytes 417800 | tf_op jit(solution)/shard_map/ppermute | solution.py:353
  7.4 0.0 collective-permute-done.1.before
  7.4 0.0 copy-done
  7.4 0.0 copy-done.2
  7.5 0.0 copy-done.1
  7.5 0.9 %shard_map.65 = (f32[8,32,128]{2,1,0:T(8,128)S(1)}, f32[6,32,256]{2,1,0:T(8,128)S(1)}, f32[8,128]{1,0:T(8,128)S(1)}) custom-call(s32[1,1]{1,0:T(1,128)S(6)} %copy.7.count, s32[1,32,256]{2,1,0:T(8,128)S(1)} %copy-done, f32[1,1,256]{2,1,0:T(1,128)S(1)} %copy-done.1, f32[1,1,256]{2,1,0:T(1,128)S(1)} %copy-done.2, f32[136,256]{1,0:T(8,128)S(1)} %collective-permute-done.1.before, ...), custom_call_target="tpu_custom_call" | custom-call | flops 10000000 | bytes 500000 | tf_op jit(solution)/shard_map/pallas_call | solution.py:327
  8.4 5.2 %collective-permute-done.after = f32[136,256]{1,0:T(8,128)S(1)} collective-permute-done((f32[136,256]{1,0:T(8,128)S(1)}, f32[136,256]{1,0:T(8,128)S(1)}, u32[]{:S(2)}, u32[]{:S(2)}) %collective-permute-start) | collective-permute-done | bytes 139296 | tf_op jit(solution)/shard_map/ppermute | solution.py:353
  13.6 0.6 shard_map.66
  14.1 12.7 %all_to_all.10 = f32[8,32,256]{2,1,0:T(8,128)S(1)} all-to-all(f32[8,32,256]{2,1,0:T(8,128)S(1)} %shard_map.66), channel_id=1, replica_groups={{0,16,32,48,64,80,96,112},{128,144,160,176,192,208,224,240},{256,272,28..., dimensions={0} | all-to-all | bytes 524288 | tf_op jit(solution)/shard_map/all_to_all | solution.py:367
  26.9 0.5 shard_map.67
  27.4 9.7 %all-gather = f32[144,128]{1,0:T(8,128)S(1)} all-gather(f32[72,128]{1,0:T(8,128)S(1)} %shard_map.67), channel_id=2, replica_groups={{0,128},{16,144},{32,160},{48,176},{64,192},{80,208},{96,224},{112,240}..., dimensions={0}, use_global_device_ids=true | all-gather | bytes 110592 | tf_op jit(solution)/shard_map/all_gather | solution.py:372
  37.1 10.7 %all-gather.1 = f32[160,128]{1,0:T(8,128)S(1)} all-gather(f32[80,128]{1,0:T(8,128)S(1)} %pad_maximum_fusion), channel_id=3, replica_groups={{0,384},{16,400},{32,416},{48,432},{64,448},{80,464},{96,480},{112,496}..., dimensions={0}, use_global_device_ids=true | all-gather | bytes 122880 | tf_op jit(solution)/shard_map/all_gather | solution.py:372
  47.8 2.7 %shard_map.68 = f32[256,256]{1,0:T(8,128)S(1)} custom-call(f32[2,80,128]{2,1,0:T(8,128)S(1)} %bitcast.13, f32[256,256]{1,0:T(8,128)S(1)} %bitcast.11), custom_call_target="tpu_custom_call" | custom-call | flops 1000000 | bytes 500000 | tf_op jit(solution)/shard_map/pallas_call | solution.py:327
  50.6 12.2 %all_to_all.11.arrived = f32[8,32,256]{2,1,0:T(8,128)S(1)} all-to-all(f32[8,32,256]{2,1,0:T(8,128)S(1)} %bitcast.12), channel_id=1, replica_groups={{0,16,32,48,64,80,96,112},{128,144,160,176,192,208,224,240},{256,272,28..., dimensions={0} | all-to-all | bytes 524288 | tf_op jit(solution)/shard_map/all_to_all | solution.py:380
  62.8 0.9 %shard_map.69 = f32[32,8,256]{2,1,0:T(8,128)} custom-call(f32[8,32,256]{2,1,0:T(8,128)S(1)} %all_to_all.11.arrived), custom_call_target="tpu_custom_call" | custom-call | flops 1000000 | bytes 500000 | tf_op jit(solution)/shard_map/pallas_call | solution.py:327
  (3 shorter events, 0.0 us)
Async XLA Ops:
  0.0 7.4 %copy-start = (s32[1,32,256]{2,1,0:T(8,128)S(1)}, s32[1,32,256]{2,1,0:T(8,128)}, u32[]{:S(2)}) copy-start(s32[1,32,256]{2,1,0:T(8,128)} %cells.1) | copy-start | bytes 98308
  1.1 6.4 %collective-permute-start.1 = (f32[136,256]{1,0:T(8,128)S(1)}, f32[136,256]{1,0:T(8,128)S(1)}, u32[]{:S(2)}, u32[]{:S(2)}) collective-permute-start(f32[136,256]{1,0:T(8,128)S(1)} %get-tuple-element.10.bottom), channel_id=1, source_target_pairs={{0,1},{1,2},{2,3},{3,4},{4,5},{5,6},{6,7},{7,8},{8,9},{9,10},{10,1... | collective-permute-start | bytes 417800 | tf_op jit(solution)/shard_map/ppermute | solution.py:352
  5.4 2.0 %copy-start.2 = (f32[1,1,256]{2,1,0:T(1,128)S(1)}, f32[1,1,256]{2,1,0:T(1,128)}, u32[]{:S(2)}) copy-start(f32[1,1,256]{2,1,0:T(1,128)} %variances.1) | copy-start | bytes 3076
  5.5 2.0 %copy-start.1 = (f32[1,1,256]{2,1,0:T(1,128)S(1)}, f32[1,1,256]{2,1,0:T(1,128)}, u32[]{:S(2)}) copy-start(f32[1,1,256]{2,1,0:T(1,128)} %values.1) | copy-start | bytes 3076
  5.5 8.1 %collective-permute-start = (f32[136,256]{1,0:T(8,128)S(1)}, f32[136,256]{1,0:T(8,128)S(1)}, u32[]{:S(2)}, u32[]{:S(2)}) collective-permute-start(f32[136,256]{1,0:T(8,128)S(1)} %get-tuple-element.11.top), channel_id=1, source_target_pairs={{1,0},{2,1},{3,2},{4,3},{5,4},{6,5},{7,6},{8,7},{9,8},{10,9},{11,1... | collective-permute-start | bytes 417800 | tf_op jit(solution)/shard_map/ppermute | solution.py:353
